TPU v7x, 32 devices: a whole 2x2x4 slice. The times are simulated.
32 devices in a mesh: fsdp: 8 (over y, x, core), tp: 4 (over z).
Axes of the slice: x: 2, y: 2, z: 4, core: 2. Of those that a mesh axis runs over, the one named last changes fastest.
Arguments:
- partials: bfloat16 [8, 2, 5120, 1024], P('fsdp', None, None, 'tp'), may hold values from -6 to 6
- token_counts: int32 [8], P('fsdp'), may hold values from 100 to 599
- owner_map: int32 [2, 4], replicated, may hold values from 0 to 3, each once within a row
- params: float32 [2, 5120, 1024], P(None, 'fsdp', 'tp'), may hold values from -0.75 to 0.75
- moment1: float32 [2, 5120, 1024], P(None, 'fsdp', 'tp'), may hold values from -0.15625 to 0.15625
- moment2: float32 [2, 5120, 1024], P(None, 'fsdp', 'tp'), may hold values from 0.0001 to 0.004
Outputs:
- new_params: float32 [2, 5120, 1024], P(None, 'fsdp', 'tp')
- new_moment1: float32 [2, 5120, 1024], P(None, 'fsdp', 'tp')
- new_moment2: float32 [2, 5120, 1024], P(None, 'fsdp', 'tp')
- rollout_delta: bfloat16 [2, 5120, 1024], P(None, None, 'tp')
Inputs may be any that keep to these rules, and one draw needn't show every extreme that they name: `owner_map`: each row is a permutation of 0 to 3.
All inputs are finite; a program needn't handle non-finite values.
Results may differ from a plain program's by a relative error of at most 0.0004.
Values may be sent and summed in bfloat16 or wider, within the bound.
A program may use at most 64 MiB of HBM per device.

v0:
```python
import functools

import jax
import jax.numpy as jnp
from jax import lax
from jax.experimental import pallas as pl
from jax.experimental.pallas import tpu as pltpu
from jax.sharding import PartitionSpec as P

STEP = 10
MESH = pl.DeviceIdType.MESH
SPLIT = 8
TILE = 16
SPAN = 80


def plain(partials, token_counts, owner_map, params, moment1, moment2):
    weight = token_counts.astype(jnp.float32)[0]
    total = lax.psum(weight, "fsdp")
    summed = lax.psum_scatter(
        weight * partials[0].astype(jnp.float32), "fsdp", scatter_dimension=1, tiled=True
    )
    first, second, direction, new_params = adam(summed * (1.0 / total), params, moment1, moment2)
    delta = direction.astype(jnp.bfloat16)
    owners = lax.axis_size("tp")
    served = lax.dynamic_index_in_dim(owner_map, lax.axis_index("tp"), 1, keepdims=False)
    blocks = lax.all_gather(delta, "tp", axis=0)
    kept = jnp.take_along_axis(blocks, served[None, :, None, None], axis=0)[0]
    rollout = lax.all_gather(kept, "fsdp", axis=1, tiled=True)
    return (new_params, first, second, rollout)


def adam(grad, params, moment1, moment2):
    first = 0.9 * moment1 + 0.1 * grad
    second = 0.999 * moment2 + 0.001 * grad * grad
    scale_one = 1.0 / (1.0 - 0.9**STEP)
    scale_two = 1.0 / (1.0 - 0.999**STEP)
    direction = first * scale_one / (jnp.sqrt(second * scale_two) + 1e-08)
    new_params = params - 0.001 * (direction + 0.1 * params)
    return first, second, direction, new_params


def kernel(
    sizes,
    owner_ref,
    w_ref,
    part_ref,
    p_ref,
    m_ref,
    v_ref,
    np_ref,
    nm_ref,
    nv_ref,
    roll_ref,
    wbuf,
    mine,
    theirs,
    acc,
    recv,
    held,
    cross,
    w_s,
    w_r,
    opt_s,
    ld_s,
    raw_s,
    raw_r,
    rs_s,
    rs_r,
    z_s,
    z_r,
    ag_s,
    ag_r,
    fin_s,
    fin_r,
):
    layers, fsdp, tp, parts, rows = sizes
    chunks = layers * parts
    pairs = fsdp // 2
    bits = pairs.bit_length() - 1
    me = lax.axis_index("fsdp")
    col = lax.axis_index("tp")
    core = lax.rem(me, 2)
    mine_q = me // 2
    partner = mine_q * 2 + (1 - core)

    def away(index, flips):
        q = index
        for b in flips:
            q = q + (1 - 2 * lax.rem(index // (1 << b), 2)) * (1 << b)
        return q

    def ones(number):
        return [b for b in range(number.bit_length()) if number >> b & 1]

    tp_bits = tp.bit_length() - 1
    barrier = pltpu.get_barrier_semaphore()
    for d in range(1, fsdp):
        pl.semaphore_signal(
            barrier, inc=1, device_id={"fsdp": lax.rem(me + d, fsdp)}, device_id_type=MESH
        )
    for b in range(tp_bits):
        pl.semaphore_signal(
            barrier, inc=1, device_id={"tp": away(col, [b])}, device_id_type=MESH
        )

    def where(c):
        return c // parts, c % parts

    loads = []
    for c in range(chunks):
        l, k = where(c)
        load = pltpu.make_async_copy(part_ref.at[l, :, core, k], mine.at[c], ld_s.at[c])
        load.start()
        loads.append(load)
    pl.semaphore_wait(barrier, fsdp - 1 + tp_bits)

    def push(src, dst, send, arrive, **device):
        copy = pltpu.make_async_remote_copy(
            src_ref=src,
            dst_ref=dst,
            send_sem=send,
            recv_sem=arrive,
            device_id=device,
            device_id_type=MESH,
        )
        copy.start()
        return copy

    weights = [push(w_ref, wbuf.at[0], w_s.at[0], w_r.at[0], fsdp=partner)]
    raws = []
    for c in range(chunks):
        l, k = where(c)
        raws.append(
            push(
                part_ref.at[l, :, 1 - core, k],
                theirs.at[c],
                raw_s.at[c],
                raw_r.at[c],
                fsdp=partner,
            )
        )
    for d in range(1, fsdp):
        weights.append(
            push(w_ref, wbuf.at[d], w_s.at[d], w_r.at[d], fsdp=lax.rem(me + d, fsdp))
        )
    opts = []
    for i, (src, dst) in enumerate(((p_ref, np_ref), (m_ref, nm_ref), (v_ref, nv_ref))):
        load = pltpu.make_async_copy(src, dst, opt_s.at[i])
        load.start()
        opts.append(load)

    my_weight = w_ref[0:1, :]
    weights[0].wait()
    other_weight = wbuf[0, 0:1, :]

    def weigh():
        total = my_weight
        for d in range(1, fsdp):
            weights[d].wait()
            total = total + wbuf[d, 0:1, :]
        return 1.0 / total

    scale = []

    def order(c):
        names = list(range(bits))
        return names if c % 2 == 0 else names[::-1]

    def flipped(flips):
        return away(mine_q, flips)

    step = next(n for n in range(min(rows, SPAN), 0, -TILE) if rows % n == 0)

    def tiles(body):
        def run(i, carry):
            body(pl.ds(pl.multiple_of(i * step, step), step))
            return carry

        lax.fori_loop(0, rows // step, run, 0)

    halving = {}
    spread = {}
    doubling = {}

    def halve(c, i):
        half = pairs >> (i + 1)
        there = flipped([order(c)[i]]) * 2 + core
        halving[c, i] = push(
            acc.at[c, pl.ds(half, half)],
            recv.at[c, pl.ds(half, half)],
            rs_s.at[c, i],
            rs_r.at[c, i],
            fsdp=there,
        )

    def held_rows(c, pos):
        q = flipped([order(c)[b] for b in ones(pos)])
        l, k = where(c)
        return roll_ref.at[l, q, core, k]

    def double(c, j):
        there = flipped([order(c)[j]]) * 2 + core
        for pos in range(1 << j):
            block = held_rows(c, pos)
            push(block, block, ag_s.at[c, j], ag_r.at[c, j], fsdp=there)

    def await_blocks(c, count, sem):
        part = mine.at[c, pl.ds(0, count)]
        pltpu.make_async_copy(part, part, sem).wait()

    def gather_sum(c):
        loads[c].wait()
        raws[c].wait_recv()
        for pos in range(pairs - 1, -1, -1):
            q = flipped([order(c)[i] for i in range(bits) if pos >> (bits - 1 - i) & 1])

            def body(at):
                acc[c, pos, at, :] = my_weight * mine[c, q, at, :].astype(
                    jnp.float32
                ) + other_weight * theirs[c, q, at, :].astype(jnp.float32)

            tiles(body)
            if pos == pairs // 2:
                halve(c, 0)

    def add(i, c):
        halving[c, i].wait_recv()
        half = pairs >> (i + 1)
        for pos in range(half - 1, -1, -1):

            def body(at):
                acc[c, pos, at, :] = acc[c, pos, at, :] + recv[c, half + pos, at, :]

            tiles(body)
            if pos == half // 2:
                halve(c, i + 1)

    def update(c):
        l, k = where(c)
        halving[c, bits - 1].wait_recv()
        if c == 0:
            for load in opts:
                load.wait()
            scale.append(weigh())

        def body(at):
            grad = (acc[c, 0, at, :] + recv[c, 1, at, :]) * scale[0]
            first, second, direction, new_params = adam(
                grad, np_ref[l, k, at, :], nm_ref[l, k, at, :], nv_ref[l, k, at, :]
            )
            held[c, 0, at, :] = direction.astype(jnp.bfloat16)
            np_ref[l, k, at, :] = new_params
            nm_ref[l, k, at, :] = first
            nv_ref[l, k, at, :] = second

        tiles(body)
        if tp_bits > 1:
            meet(c, 0)
        else:
            hand_over(c)

    def meet(c, b):
        size = 1 << b
        spread[c, b] = push(
            held.at[c, pl.ds(0, size)],
            held.at[c, pl.ds(size, size)],
            z_s.at[c, b],
            z_r.at[c, b],
            tp=away(col, [b]),
        )

    def pick(c, at, served, start):
        kept = start
        for slot in range(tp // 2):
            kept = jnp.where(
                served == away(col, ones(slot)), held[c, slot, at, :].astype(jnp.float32), kept
            )
        return kept.astype(jnp.bfloat16)

    def hand_over(c):
        l, k = where(c)
        there = away(col, [tp_bits - 1])
        served = owner_ref[l, there]

        def body(at):
            cross[c, 0, at, :] = pick(c, at, served, held[c, 0, at, :].astype(jnp.float32))

        tiles(body)
        spread[c, tp_bits - 1] = push(
            cross.at[c, 0],
            cross.at[c, 1],
            z_s.at[c, tp_bits - 1],
            z_r.at[c, tp_bits - 1],
            tp=there,
        )

    def met(b, c):
        spread[c, b].wait_recv()
        if b + 2 < tp_bits:
            meet(c, b + 1)
        else:
            hand_over(c)

    def select(c):
        l, k = where(c)
        spread[c, tp_bits - 1].wait_recv()
        served = owner_ref[l, col]

        def body(at):
            roll_ref[l, mine_q, core, k, at, :] = pick(
                c, at, served, cross[c, 1, at, :].astype(jnp.float32)
            )

        tiles(body)
        double(c, 0)
        finish(c, 0, 1)

    def finish(c, first, count):
        for pos in range(first, first + count):
            block = held_rows(c, pos)
            push(block, block, fin_s.at[c], fin_r.at[c], fsdp=partner)

    def forward(j, c):
        await_blocks(c, 1 << j, ag_r.at[c, j])
        if j + 1 < bits:
            double(c, j + 1)
        finish(c, 1 << j, 1 << j)

    stages = [gather_sum]
    stages += [functools.partial(add, i) for i in range(bits - 1)]
    stages += [update]
    stages += [functools.partial(met, b) for b in range(tp_bits - 1)]
    stages += [select]
    stages += [functools.partial(forward, j) for j in range(bits)]
    groups = [tuple(range(c, min(c + 2, chunks))) for c in range(0, chunks, 2)]
    for t in range(len(groups) + len(stages) - 1):
        for s, stage in enumerate(stages):
            if 0 <= t - s < len(groups):
                for c in groups[t - s]:
                    stage(c)

    for c in range(chunks):
        raws[c].wait_send()
        for i in range(bits):
            halving[c, i].wait_send()
            await_blocks(c, 1 << i, ag_s.at[c, i])
        for b in range(tp_bits):
            spread[c, b].wait_send()
        for sem in (fin_s, fin_r):
            await_blocks(c, pairs, sem.at[c])


def write_out(*refs):
    count = len(refs) // 2
    copies = []
    for i in range(count):
        for l in range(refs[i].shape[0]):
            sem = refs[-1].at[i, l]
            copies.append(pltpu.make_async_copy(refs[i].at[l], refs[count + i].at[l], sem))
    for copy in copies:
        copy.start()
    for copy in copies:
        copy.wait()


def fused(fsdp, tp, partials, token_counts, owner_map, params, moment1, moment2):
    layers, depth, width = partials.shape[1:]
    per = params.shape[1]
    pairs = fsdp // 2
    bits = pairs.bit_length() - 1
    tp_bits = tp.bit_length() - 1
    parts = next(n for n in range(SPLIT, 0, -1) if per % (n * TILE) == 0)
    rows = per // parts
    chunks = layers * parts
    weight = jnp.broadcast_to(token_counts.astype(jnp.float32)[:, None], (8, width))
    anywhere = pl.BlockSpec(memory_space=pl.ANY)
    dma = pltpu.SemaphoreType.DMA
    state = (layers, parts, rows, width)
    f32, b16 = jnp.float32, jnp.bfloat16
    outs = pl.pallas_call(
        functools.partial(kernel, (layers, fsdp, tp, parts, rows)),
        out_shape=[
            pltpu.VMEM(state, f32),
            pltpu.VMEM(state, f32),
            pltpu.VMEM(state, f32),
            pltpu.VMEM((layers, pairs, 2, parts, rows, width), b16),
        ],
        in_specs=[
            pl.BlockSpec(memory_space=pltpu.SMEM),
            pl.BlockSpec(memory_space=pltpu.VMEM),
            anywhere,
            anywhere,
            anywhere,
            anywhere,
        ],
        out_specs=[pl.BlockSpec(memory_space=pltpu.VMEM)] * 4,
        scratch_shapes=[
            pltpu.VMEM((fsdp, 8, width), f32),
            pltpu.VMEM((chunks, pairs, rows, width), b16),
            pltpu.VMEM((chunks, pairs, rows, width), b16),
            pltpu.VMEM((chunks, pairs, rows, width), f32),
            pltpu.VMEM((chunks, pairs, rows, width), f32),
            pltpu.VMEM((chunks, tp // 2, rows, width), b16),
            pltpu.VMEM((chunks, 2, rows, width), b16),
            dma((fsdp,)),
            dma((fsdp,)),
            dma((3,)),
            dma((chunks,)),
            dma((chunks,)),
            dma((chunks,)),
            dma((chunks, bits)),
            dma((chunks, bits)),
            dma((chunks, tp_bits)),
            dma((chunks, tp_bits)),
            dma((chunks, bits)),
            dma((chunks, bits)),
            dma((chunks,)),
            dma((chunks,)),
        ],
        compiler_params=pltpu.CompilerParams(
            collective_id=0, has_side_effects=True, vmem_limit_bytes=48 * 1024 * 1024
        ),
    )(
        owner_map,
        weight,
        partials.reshape(layers, pairs, 2, parts, rows, width),
        params.reshape(state),
        moment1.reshape(state),
        moment2.reshape(state),
    )
    outs = [out.reshape(params.shape) for out in outs[:3]] + [outs[3].reshape(layers, depth, width)]
    return tuple(
        pl.pallas_call(
            write_out,
            out_shape=[jax.ShapeDtypeStruct(out.shape, out.dtype) for out in outs],
            in_specs=[pl.BlockSpec(memory_space=pltpu.VMEM)] * 4,
            out_specs=[anywhere] * 4,
            scratch_shapes=[dma((4, layers))],
            compiler_params=pltpu.CompilerParams(vmem_limit_bytes=16 * 1024 * 1024),
        )(*outs)
    )


def solution(mesh):
    fsdp, tp = mesh.shape["fsdp"], mesh.shape["tp"]
    local = plain
    if fsdp >= 4 and fsdp & (fsdp - 1) == 0 and tp > 1 and tp & (tp - 1) == 0:
        local = functools.partial(fused, fsdp, tp)
    in_specs = (
        P("fsdp", None, None, "tp"),
        P("fsdp"),
        P(),
        P(None, "fsdp", "tp"),
        P(None, "fsdp", "tp"),
        P(None, "fsdp", "tp"),
    )
    out_specs = (
        P(None, "fsdp", "tp"),
        P(None, "fsdp", "tp"),
        P(None, "fsdp", "tp"),
        P(None, None, "tp"),
    )
    return jax.shard_map(local, mesh=mesh, in_specs=in_specs, out_specs=out_specs, check_vma=False)
```

profile of v0, /device:TPU:0, one launch (start us, length us, event | category | flops | bytes accessed | tf_op | source)
XLA Modules:
  0.0 85.9 jit_solution(3483593486297903058)
XLA Ops:
  1.3 0.6 broadcast_in_dim.9.w_ref
  1.9 80.3 %shard_map.93 = (f32[2,8,80,256]{3,2,1,0:T(8,128)S(1)}, f32[2,8,80,256]{3,2,1,0:T(8,128)S(1)}, f32[2,8,80,256]{3,2,1,0:T(8,128)S(1)}, bf16[2,4,2,8,80,256]{5,4,3,2,1,0:T(8,128)(2,1)S(1)}) custom-call(s32[2,4]{1,0:T(2,128)} %owner_ref.1, f32[8,256]{1,0:T(8,128)} %broadcast_in_dim.9.w_ref, bf16[2,4,2,8,80,256]{5,4,3,2,1,0:T(8,128)(2,1)} %bitcast.13, ...), custom_call_target="tpu_custom_call" | custom-call | tf_op jit(solution)/shard_map/pallas_call | solution.py:381
  82.1 3.7 %shard_map.94 = (f32[2,640,256]{2,1,0:T(8,128)}, f32[2,640,256]{2,1,0:T(8,128)}, f32[2,640,256]{2,1,0:T(8,128)}, bf16[2,5120,256]{2,1,0:T(8,128)(2,1)}) custom-call(f32[2,640,256]{2,1,0:T(8,128)S(1)} %bitcast.10, f32[2,640,256]{2,1,0:T(8,128)S(1)} %bitcast.11, f32[2,640,256]{2,1,0:T(8,128)S(1)} %bitcast.12, bf16[2,5120,256]{2,1,0:T(8,128)(2,1)S(1)} %bitcast.9), custom_call_target="tpu_custom_call" | custom-call | tf_op jit(solution)/shard_map/pallas_call | solution.py:434
where the time goes:
time: 86.1 us; the launch traced here: 85.9 us
  Pallas kernels  84 us (98%)
  between operations  1.29 us (1%)
    pallas_call x1, Pallas kernels, fused(): pl.pallas_call(functools.partial(kernel, (layers, fsdp, tp, parts, rows))...  80.3 us
    pallas_call x1, Pallas kernels, fused(): pl.pallas_call(write_out, out_shape=[jax.ShapeDtypeStruct(out.shape, out....  3.72 us

commit v1 on v0

--- a/solution.py
+++ b/solution.py
@@ -12,6 +12,8 @@
 SPLIT = 8
 TILE = 16
 SPAN = 80
+AHEAD = 2
+LATE = 3
 
 
 def plain(partials, token_counts, owner_map, params, moment1, moment2):
@@ -43,7 +45,7 @@
 def kernel(
     sizes,
     owner_ref,
-    w_ref,
+    count_ref,
     part_ref,
     p_ref,
     m_ref,
@@ -52,9 +54,11 @@
     nm_ref,
     nv_ref,
     roll_ref,
+    own_w,
     wbuf,
     mine,
     theirs,
+    near,
     acc,
     recv,
     held,
@@ -65,6 +69,8 @@
     ld_s,
     raw_s,
     raw_r,
+    near_s,
+    near_r,
     rs_s,
     rs_r,
     z_s,
@@ -77,6 +83,7 @@
     layers, fsdp, tp, parts, rows = sizes
     chunks = layers * parts
     pairs = fsdp // 2
+    kept = pairs // 2
     bits = pairs.bit_length() - 1
     me = lax.axis_index("fsdp")
     col = lax.axis_index("tp")
@@ -107,12 +114,23 @@
     def where(c):
         return c // parts, c % parts
 
-    loads = []
+    def order(c):
+        names = list(range(bits))
+        return names if c % 2 == 0 else names[::-1]
+
+    def flipped(flips):
+        return away(mine_q, flips)
+
+    def block_of(c, pos):
+        return flipped([order(c)[i] for i in range(bits) if pos >> (bits - 1 - i) & 1])
+
+    own_w[...] = jnp.full(own_w.shape, count_ref[0], jnp.int32).astype(jnp.float32)
     for c in range(chunks):
         l, k = where(c)
-        load = pltpu.make_async_copy(part_ref.at[l, :, core, k], mine.at[c], ld_s.at[c])
-        load.start()
-        loads.append(load)
+        for pos in range(kept):
+            pltpu.make_async_copy(
+                part_ref.at[l, block_of(c, pos), core, k], mine.at[c, pos], ld_s.at[c]
+            ).start()
     pl.semaphore_wait(barrier, fsdp - 1 + tp_bits)
 
     def push(src, dst, send, arrive, **device):
@@ -127,48 +145,71 @@
         copy.start()
         return copy
 
-    weights = [push(w_ref, wbuf.at[0], w_s.at[0], w_r.at[0], fsdp=partner)]
-    raws = []
-    for c in range(chunks):
-        l, k = where(c)
-        raws.append(
+    weights = []
+    for d in range(1, fsdp):
+        weights.append(
+            push(own_w, wbuf.at[d], w_s.at[d], w_r.at[d], fsdp=lax.rem(me + d, fsdp))
+        )
+
+    def pass_on(c):
+        l, k = where(c)
+        there = flipped([order(c)[0]])
+        for pos in range(kept):
+            for half in range(2):
+                push(
+                    part_ref.at[l, block_of(c, kept + pos), half, k],
+                    near.at[c, core, pos],
+                    near_s.at[c],
+                    near_r.at[c],
+                    fsdp=there * 2 + half,
+                )
+
+    def share(c):
+        l, k = where(c)
+        for pos in range(kept):
             push(
-                part_ref.at[l, :, 1 - core, k],
-                theirs.at[c],
+                part_ref.at[l, block_of(c, pos), 1 - core, k],
+                theirs.at[c, pos],
                 raw_s.at[c],
                 raw_r.at[c],
                 fsdp=partner,
             )
-        )
-    for d in range(1, fsdp):
-        weights.append(
-            push(w_ref, wbuf.at[d], w_s.at[d], w_r.at[d], fsdp=lax.rem(me + d, fsdp))
-        )
+
+    groups = [tuple(range(c, min(c + 2, chunks))) for c in range(0, chunks, 2)]
+    for group in groups[:AHEAD]:
+        for c in group:
+            share(c)
+            pass_on(c)
+    for group in groups[AHEAD:]:
+        for c in group:
+            share(c)
     opts = []
     for i, (src, dst) in enumerate(((p_ref, np_ref), (m_ref, nm_ref), (v_ref, nv_ref))):
         load = pltpu.make_async_copy(src, dst, opt_s.at[i])
         load.start()
         opts.append(load)
 
-    my_weight = w_ref[0:1, :]
-    weights[0].wait()
-    other_weight = wbuf[0, 0:1, :]
+    lanes = own_w.shape[1]
+    width = mine.shape[3]
+
+    def row(tile):
+        return jnp.concatenate([tile[0:1, :]] * (width // lanes), axis=1)
+
+    my_weight = row(own_w[...])
+    met_weights = []
+
+    def weight_of(index):
+        return row(wbuf[lax.rem(me - index + fsdp, fsdp)])
 
     def weigh():
         total = my_weight
         for d in range(1, fsdp):
-            weights[d].wait()
-            total = total + wbuf[d, 0:1, :]
-        return 1.0 / total
-
-    scale = []
-
-    def order(c):
-        names = list(range(bits))
-        return names if c % 2 == 0 else names[::-1]
-
-    def flipped(flips):
-        return away(mine_q, flips)
+            weights[d - 1].wait()
+            total = total + row(wbuf[d])
+        met_weights.append(1.0 / total)
+        met_weights.append(weight_of(partner))
+        for b in range(bits):
+            met_weights.append([weight_of(flipped([b]) * 2 + half) for half in range(2)])
 
     step = next(n for n in range(min(rows, SPAN), 0, -TILE) if rows % n == 0)
 
@@ -181,7 +222,6 @@
 
     halving = {}
     spread = {}
-    doubling = {}
 
     def halve(c, i):
         half = pairs >> (i + 1)
@@ -205,24 +245,35 @@
             block = held_rows(c, pos)
             push(block, block, ag_s.at[c, j], ag_r.at[c, j], fsdp=there)
 
+    def await_part(part, sem):
+        pltpu.make_async_copy(part, part, sem).wait()
+
     def await_blocks(c, count, sem):
-        part = mine.at[c, pl.ds(0, count)]
-        pltpu.make_async_copy(part, part, sem).wait()
+        l, k = where(c)
+        await_part(near.at[c, 0, pl.ds(0, count)], sem)
 
     def gather_sum(c):
-        loads[c].wait()
-        raws[c].wait_recv()
-        for pos in range(pairs - 1, -1, -1):
-            q = flipped([order(c)[i] for i in range(bits) if pos >> (bits - 1 - i) & 1])
+        await_part(mine.at[c], ld_s.at[c])
+        await_part(theirs.at[c], raw_r.at[c])
+        await_part(near.at[c], near_r.at[c])
+        if c == 0:
+            weigh()
+        other_weight = met_weights[1]
+        near_weights = met_weights[2 + order(c)[0]]
+        for pos in range(kept - 1, -1, -1):
 
             def body(at):
-                acc[c, pos, at, :] = my_weight * mine[c, q, at, :].astype(
-                    jnp.float32
-                ) + other_weight * theirs[c, q, at, :].astype(jnp.float32)
+                total = my_weight * mine[c, pos, at, :].astype(jnp.float32)
+                total = total + other_weight * theirs[c, pos, at, :].astype(jnp.float32)
+                for half in range(2):
+                    total = total + near_weights[half] * near[c, half, pos, at, :].astype(
+                        jnp.float32
+                    )
+                acc[c, pos, at, :] = total
 
             tiles(body)
-            if pos == pairs // 2:
-                halve(c, 0)
+            if bits > 1 and pos == kept // 2:
+                halve(c, 1)
 
     def add(i, c):
         halving[c, i].wait_recv()
@@ -238,16 +289,19 @@
 
     def update(c):
         l, k = where(c)
-        halving[c, bits - 1].wait_recv()
+        if bits > 1:
+            halving[c, bits - 1].wait_recv()
         if c == 0:
             for load in opts:
                 load.wait()
-            scale.append(weigh())
+        scale = met_weights[0]
 
         def body(at):
-            grad = (acc[c, 0, at, :] + recv[c, 1, at, :]) * scale[0]
+            total = acc[c, 0, at, :]
+            if bits > 1:
+                total = total + recv[c, 1, at, :]
             first, second, direction, new_params = adam(
-                grad, np_ref[l, k, at, :], nm_ref[l, k, at, :], nv_ref[l, k, at, :]
+                total * scale, np_ref[l, k, at, :], nm_ref[l, k, at, :], nv_ref[l, k, at, :]
             )
             held[c, 0, at, :] = direction.astype(jnp.bfloat16)
             np_ref[l, k, at, :] = new_params
@@ -271,12 +325,12 @@
         )
 
     def pick(c, at, served, start):
-        kept = start
+        chosen = start
         for slot in range(tp // 2):
-            kept = jnp.where(
-                served == away(col, ones(slot)), held[c, slot, at, :].astype(jnp.float32), kept
+            chosen = jnp.where(
+                served == away(col, ones(slot)), held[c, slot, at, :].astype(jnp.float32), chosen
             )
-        return kept.astype(jnp.bfloat16)
+        return chosen.astype(jnp.bfloat16)
 
     def hand_over(c):
         l, k = where(c)
@@ -328,27 +382,33 @@
         finish(c, 1 << j, 1 << j)
 
     stages = [gather_sum]
-    stages += [functools.partial(add, i) for i in range(bits - 1)]
+    stages += [functools.partial(add, i) for i in range(1, bits - 1)]
     stages += [update]
     stages += [functools.partial(met, b) for b in range(tp_bits - 1)]
-    stages += [select]
-    stages += [functools.partial(forward, j) for j in range(bits)]
-    groups = [tuple(range(c, min(c + 2, chunks))) for c in range(0, chunks, 2)]
-    for t in range(len(groups) + len(stages) - 1):
-        for s, stage in enumerate(stages):
-            if 0 <= t - s < len(groups):
-                for c in groups[t - s]:
+    lags = list(range(len(stages)))
+    tail = [select] + [functools.partial(forward, j) for j in range(bits)]
+    lags += [len(stages) + LATE + i for i in range(len(tail))]
+    stages += tail
+    for t in range(len(groups) + lags[-1]):
+        for lag, stage in zip(lags, stages):
+            if 0 <= t - lag < len(groups):
+                for c in groups[t - lag]:
                     stage(c)
+            if lag == 0 and t + AHEAD < len(groups):
+                for c in groups[t + AHEAD]:
+                    pass_on(c)
 
     for c in range(chunks):
-        raws[c].wait_send()
+        await_part(theirs.at[c], raw_s.at[c])
+        await_part(near.at[c], near_s.at[c])
+        for i in range(1, bits):
+            halving[c, i].wait_send()
         for i in range(bits):
-            halving[c, i].wait_send()
             await_blocks(c, 1 << i, ag_s.at[c, i])
         for b in range(tp_bits):
             spread[c, b].wait_send()
         for sem in (fin_s, fin_r):
-            await_blocks(c, pairs, sem.at[c])
+            await_part(roll_ref.at[0, :, 0, 0], sem.at[c])
 
 
 def write_out(*refs):
@@ -373,7 +433,7 @@
     parts = next(n for n in range(SPLIT, 0, -1) if per % (n * TILE) == 0)
     rows = per // parts
     chunks = layers * parts
-    weight = jnp.broadcast_to(token_counts.astype(jnp.float32)[:, None], (8, width))
+    lanes = 128 if width % 128 == 0 else width
     anywhere = pl.BlockSpec(memory_space=pl.ANY)
     dma = pltpu.SemaphoreType.DMA
     state = (layers, parts, rows, width)
@@ -388,7 +448,7 @@
         ],
         in_specs=[
             pl.BlockSpec(memory_space=pltpu.SMEM),
-            pl.BlockSpec(memory_space=pltpu.VMEM),
+            pl.BlockSpec(memory_space=pltpu.SMEM),
             anywhere,
             anywhere,
             anywhere,
@@ -396,16 +456,20 @@
         ],
         out_specs=[pl.BlockSpec(memory_space=pltpu.VMEM)] * 4,
         scratch_shapes=[
-            pltpu.VMEM((fsdp, 8, width), f32),
-            pltpu.VMEM((chunks, pairs, rows, width), b16),
-            pltpu.VMEM((chunks, pairs, rows, width), b16),
-            pltpu.VMEM((chunks, pairs, rows, width), f32),
-            pltpu.VMEM((chunks, pairs, rows, width), f32),
+            pltpu.VMEM((8, lanes), f32),
+            pltpu.VMEM((fsdp, 8, lanes), f32),
+            pltpu.VMEM((chunks, pairs // 2, rows, width), b16),
+            pltpu.VMEM((chunks, pairs // 2, rows, width), b16),
+            pltpu.VMEM((chunks, 2, pairs // 2, rows, width), b16),
+            pltpu.VMEM((chunks, pairs // 2, rows, width), f32),
+            pltpu.VMEM((chunks, pairs // 2, rows, width), f32),
             pltpu.VMEM((chunks, tp // 2, rows, width), b16),
             pltpu.VMEM((chunks, 2, rows, width), b16),
             dma((fsdp,)),
             dma((fsdp,)),
             dma((3,)),
+            dma((chunks,)),
+            dma((chunks,)),
             dma((chunks,)),
             dma((chunks,)),
             dma((chunks,)),
@@ -423,7 +487,7 @@
         ),
     )(
         owner_map,
-        weight,
+        token_counts,
         partials.reshape(layers, pairs, 2, parts, rows, width),
         params.reshape(state),
         moment1.reshape(state),

time: 86.1 us -> 83.6 us (0.971)
  Pallas kernels: 84 us -> 82.2 us
    pallas_call x1, Pallas kernels: 80.3 us -> 78.5 us  [fused(): pl.pallas_call(functools.partial(kernel, (layers, fsdp, tp, parts, rows))...]
where the time goes in v1:
time: 83.6 us; the launch traced here: 83.5 us
  Pallas kernels  82.2 us (98%)
  between operations  1.29 us (2%)
    pallas_call x1, Pallas kernels, fused(): pl.pallas_call(functools.partial(kernel, (layers, fsdp, tp, parts, rows))...  78.5 us
    pallas_call x1, Pallas kernels, fused(): pl.pallas_call(write_out, out_shape=[jax.ShapeDtypeStruct(out.shape, out....  3.72 us

profile of v1, /device:TPU:0, one launch (start us, length us, event | category | flops | bytes accessed | tf_op | source)
XLA Modules:
  0.0 83.5 jit_solution(602280288797709833)
XLA Ops:
  1.3 78.5 %shard_map.93 = (f32[2,8,80,256]{3,2,1,0:T(8,128)S(1)}, f32[2,8,80,256]{3,2,1,0:T(8,128)S(1)}, f32[2,8,80,256]{3,2,1,0:T(8,128)S(1)}, bf16[2,4,2,8,80,256]{5,4,3,2,1,0:T(8,128)(2,1)S(1)}) custom-call(s32[2,4]{1,0:T(2,128)} %owner_ref.1, s32[1]{0:T(128)S(6)} %copy.10.count_ref, bf16[2,4,2,8,80,256]{5,4,3,2,1,0:T(8,128)(2,1)} %bitcast.12, ...), custom_call_target="tpu_custom_call" | custom-call | tf_op jit(solution)/shard_map/pallas_call | solution.py:441
  79.7 3.7 %shard_map.94 = (f32[2,640,256]{2,1,0:T(8,128)}, f32[2,640,256]{2,1,0:T(8,128)}, f32[2,640,256]{2,1,0:T(8,128)}, bf16[2,5120,256]{2,1,0:T(8,128)(2,1)}) custom-call(f32[2,640,256]{2,1,0:T(8,128)S(1)} %bitcast.9, f32[2,640,256]{2,1,0:T(8,128)S(1)} %bitcast.10, f32[2,640,256]{2,1,0:T(8,128)S(1)} %bitcast.11, bf16[2,5120,256]{2,1,0:T(8,128)(2,1)S(1)} %bitcast.8), custom_call_target="tpu_custom_call" | custom-call | tf_op jit(solution)/shard_map/pallas_call | solution.py:498

commit v2 on v0

--- a/solution.py
+++ b/solution.py
@@ -9,9 +9,13 @@
 
 STEP = 10
 MESH = pl.DeviceIdType.MESH
-SPLIT = 8
+SPLIT = 10
 TILE = 16
 SPAN = 80
+AHEAD = 2
+LATE = 2
+LEVELS = 127
+FINE = LEVELS * 256
 
 
 def plain(partials, token_counts, owner_map, params, moment1, moment2):
@@ -40,10 +44,19 @@
     return first, second, direction, new_params
 
 
+def code(value, high):
+    rest = jnp.where(high == 0.0, 0.0, (value - high) * FINE / high)
+    return (rest + (LEVELS + 1.5)).astype(jnp.int32)
+
+
+def decode(high, number):
+    return high + (number.astype(jnp.float32) - (LEVELS + 1.0)) * (high * (1.0 / FINE))
+
+
 def kernel(
     sizes,
     owner_ref,
-    w_ref,
+    count_ref,
     part_ref,
     p_ref,
     m_ref,
@@ -52,11 +65,15 @@
     nm_ref,
     nv_ref,
     roll_ref,
+    own_w,
     wbuf,
     mine,
     theirs,
+    out_hi,
+    out_lo,
+    in_hi,
+    in_lo,
     acc,
-    recv,
     held,
     cross,
     w_s,
@@ -65,8 +82,10 @@
     ld_s,
     raw_s,
     raw_r,
-    rs_s,
-    rs_r,
+    hi_s,
+    hi_r,
+    lo_s,
+    lo_r,
     z_s,
     z_r,
     ag_s,
@@ -77,6 +96,7 @@
     layers, fsdp, tp, parts, rows = sizes
     chunks = layers * parts
     pairs = fsdp // 2
+    kept = pairs // 2
     bits = pairs.bit_length() - 1
     me = lax.axis_index("fsdp")
     col = lax.axis_index("tp")
@@ -107,6 +127,17 @@
     def where(c):
         return c // parts, c % parts
 
+    def order(c):
+        names = list(range(bits))
+        return names if c % 2 == 0 else names[::-1]
+
+    def flipped(flips):
+        return away(mine_q, flips)
+
+    def block_of(c, pos):
+        return flipped([order(c)[i] for i in range(bits) if pos >> (bits - 1 - i) & 1])
+
+    own_w[...] = jnp.full(own_w.shape, count_ref[0], jnp.int32).astype(jnp.float32)
     loads = []
     for c in range(chunks):
         l, k = where(c)
@@ -127,7 +158,11 @@
         copy.start()
         return copy
 
-    weights = [push(w_ref, wbuf.at[0], w_s.at[0], w_r.at[0], fsdp=partner)]
+    weights = [None] * fsdp
+
+    groups = [tuple(range(c, min(c + 2, chunks))) for c in range(0, chunks, 2)]
+    for d in range(1, fsdp):
+        weights[d] = push(own_w, wbuf.at[d], w_s.at[d], w_r.at[d], fsdp=lax.rem(me + d, fsdp))
     raws = []
     for c in range(chunks):
         l, k = where(c)
@@ -140,37 +175,31 @@
                 fsdp=partner,
             )
         )
-    for d in range(1, fsdp):
-        weights.append(
-            push(w_ref, wbuf.at[d], w_s.at[d], w_r.at[d], fsdp=lax.rem(me + d, fsdp))
-        )
     opts = []
     for i, (src, dst) in enumerate(((p_ref, np_ref), (m_ref, nm_ref), (v_ref, nv_ref))):
         load = pltpu.make_async_copy(src, dst, opt_s.at[i])
         load.start()
         opts.append(load)
 
-    my_weight = w_ref[0:1, :]
-    weights[0].wait()
-    other_weight = wbuf[0, 0:1, :]
+    lanes = own_w.shape[1]
+    width = mine.shape[3]
+
+    def row(tile):
+        return jnp.concatenate([tile[0:1, :]] * (width // lanes), axis=1)
+
+    my_weight = row(own_w[...])
+    all_weights = []
 
     def weigh():
         total = my_weight
         for d in range(1, fsdp):
             weights[d].wait()
-            total = total + wbuf[d, 0:1, :]
-        return 1.0 / total
-
-    scale = []
-
-    def order(c):
-        names = list(range(bits))
-        return names if c % 2 == 0 else names[::-1]
-
-    def flipped(flips):
-        return away(mine_q, flips)
-
-    step = next(n for n in range(min(rows, SPAN), 0, -TILE) if rows % n == 0)
+            total = total + row(wbuf[d])
+        all_weights.append(row(wbuf[lax.rem(me - partner + fsdp, fsdp)]))
+        all_weights.append(1.0 / total)
+
+    side = rows // 2
+    step = next(n for n in range(min(side, SPAN), 0, -TILE) if side % n == 0)
 
     def tiles(body):
         def run(i, carry):
@@ -179,20 +208,66 @@
 
         lax.fori_loop(0, rows // step, run, 0)
 
+    def quads(body):
+        def run(i, carry):
+            start = pl.multiple_of(i * step, step)
+            body(pl.ds(start, step), pl.ds(pl.multiple_of(start + side, step), step))
+            return carry
+
+        lax.fori_loop(0, side // step, run, 0)
+
     halving = {}
     spread = {}
-    doubling = {}
 
     def halve(c, i):
         half = pairs >> (i + 1)
         there = flipped([order(c)[i]]) * 2 + core
-        halving[c, i] = push(
-            acc.at[c, pl.ds(half, half)],
-            recv.at[c, pl.ds(half, half)],
-            rs_s.at[c, i],
-            rs_r.at[c, i],
-            fsdp=there,
-        )
+        halving[c, i] = [
+            push(
+                src.at[c, pl.ds(half, half)],
+                dst.at[c, pl.ds(half, half)],
+                send.at[c, i],
+                arrive.at[c, i],
+                fsdp=there,
+            )
+            for src, dst, send, arrive in (
+                (out_hi, in_hi, hi_s, hi_r),
+                (out_lo, in_lo, lo_s, lo_r),
+            )
+        ]
+
+    def arrived(c, i):
+        for copy in halving[c, i]:
+            copy.wait_recv()
+
+    def pair_sum(c, pos, at):
+        q = block_of(c, pos)
+        return my_weight * mine[c, q, at, :].astype(jnp.float32) + all_weights[0] * theirs[
+            c, q, at, :
+        ].astype(jnp.float32)
+
+    def write(c, pos, at, pair, values):
+        numbers = []
+        for rows_at, value in zip(pair, values):
+            high = value.astype(jnp.bfloat16)
+            out_hi[c, pos, rows_at, :] = high
+            number = code(value, high.astype(jnp.float32))
+            numbers += [number[:, : width // 2], number[:, width // 2 :]]
+        word = numbers[0]
+        for n in range(1, 4):
+            word = word | (numbers[n] << (8 * n))
+        out_lo[c, pos, at, :] = word
+
+    def read(c, pos, at, pair):
+        word = in_lo[c, pos, at, :]
+        numbers = [(word >> (8 * n)) & 255 for n in range(4)]
+        return [
+            decode(
+                in_hi[c, pos, rows_at, :].astype(jnp.float32),
+                jnp.concatenate(numbers[2 * n : 2 * n + 2], axis=1),
+            )
+            for n, rows_at in enumerate(pair)
+        ]
 
     def held_rows(c, pos):
         q = flipped([order(c)[b] for b in ones(pos)])
@@ -205,56 +280,65 @@
             block = held_rows(c, pos)
             push(block, block, ag_s.at[c, j], ag_r.at[c, j], fsdp=there)
 
+    def await_part(part, sem):
+        pltpu.make_async_copy(part, part, sem).wait()
+
     def await_blocks(c, count, sem):
-        part = mine.at[c, pl.ds(0, count)]
-        pltpu.make_async_copy(part, part, sem).wait()
-
-    def gather_sum(c):
+        await_part(mine.at[c, pl.ds(0, count)], sem)
+
+    def first_half(c):
         loads[c].wait()
         raws[c].wait_recv()
-        for pos in range(pairs - 1, -1, -1):
-            q = flipped([order(c)[i] for i in range(bits) if pos >> (bits - 1 - i) & 1])
-
-            def body(at):
-                acc[c, pos, at, :] = my_weight * mine[c, q, at, :].astype(
-                    jnp.float32
-                ) + other_weight * theirs[c, q, at, :].astype(jnp.float32)
-
-            tiles(body)
-            if pos == pairs // 2:
-                halve(c, 0)
+        if c == 0:
+            weigh()
+        for pos in range(pairs - 1, kept - 1, -1):
+
+            def body(*pair):
+                write(c, pos, pair[0], pair, [pair_sum(c, pos, at) for at in pair])
+
+            quads(body)
+        halve(c, 0)
 
     def add(i, c):
-        halving[c, i].wait_recv()
+        arrived(c, i)
         half = pairs >> (i + 1)
         for pos in range(half - 1, -1, -1):
 
-            def body(at):
-                acc[c, pos, at, :] = acc[c, pos, at, :] + recv[c, half + pos, at, :]
-
-            tiles(body)
-            if pos == half // 2:
+            def body(*pair):
+                totals = read(c, half + pos, pair[0], pair)
+                for n, at in enumerate(pair):
+                    totals[n] += pair_sum(c, pos, at) if i == 0 else acc[c, pos, at, :]
+                if half > 1 and pos >= half // 2:
+                    write(c, pos, pair[0], pair, totals)
+                else:
+                    for at, total in zip(pair, totals):
+                        acc[c, pos, at, :] = total
+
+            quads(body)
+            if half > 1 and pos == half // 2:
                 halve(c, i + 1)
 
     def update(c):
         l, k = where(c)
-        halving[c, bits - 1].wait_recv()
+        arrived(c, bits - 1)
         if c == 0:
             for load in opts:
                 load.wait()
-            scale.append(weigh())
-
-        def body(at):
-            grad = (acc[c, 0, at, :] + recv[c, 1, at, :]) * scale[0]
-            first, second, direction, new_params = adam(
-                grad, np_ref[l, k, at, :], nm_ref[l, k, at, :], nv_ref[l, k, at, :]
-            )
-            held[c, 0, at, :] = direction.astype(jnp.bfloat16)
-            np_ref[l, k, at, :] = new_params
-            nm_ref[l, k, at, :] = first
-            nv_ref[l, k, at, :] = second
-
-        tiles(body)
+        scale = all_weights[1]
+
+        def body(*pair):
+            totals = read(c, 1, pair[0], pair)
+            for at, total in zip(pair, totals):
+                total = total + (pair_sum(c, 0, at) if bits == 1 else acc[c, 0, at, :])
+                first, second, direction, new_params = adam(
+                    total * scale, np_ref[l, k, at, :], nm_ref[l, k, at, :], nv_ref[l, k, at, :]
+                )
+                held[c, 0, at, :] = direction.astype(jnp.bfloat16)
+                np_ref[l, k, at, :] = new_params
+                nm_ref[l, k, at, :] = first
+                nv_ref[l, k, at, :] = second
+
+        quads(body)
         if tp_bits > 1:
             meet(c, 0)
         else:
@@ -271,12 +355,12 @@
         )
 
     def pick(c, at, served, start):
-        kept = start
+        chosen = start
         for slot in range(tp // 2):
-            kept = jnp.where(
-                served == away(col, ones(slot)), held[c, slot, at, :].astype(jnp.float32), kept
+            chosen = jnp.where(
+                served == away(col, ones(slot)), held[c, slot, at, :].astype(jnp.float32), chosen
             )
-        return kept.astype(jnp.bfloat16)
+        return chosen.astype(jnp.bfloat16)
 
     def hand_over(c):
         l, k = where(c)
@@ -327,28 +411,31 @@
             double(c, j + 1)
         finish(c, 1 << j, 1 << j)
 
-    stages = [gather_sum]
-    stages += [functools.partial(add, i) for i in range(bits - 1)]
-    stages += [update]
-    stages += [functools.partial(met, b) for b in range(tp_bits - 1)]
-    stages += [select]
-    stages += [functools.partial(forward, j) for j in range(bits)]
-    groups = [tuple(range(c, min(c + 2, chunks))) for c in range(0, chunks, 2)]
-    for t in range(len(groups) + len(stages) - 1):
-        for s, stage in enumerate(stages):
-            if 0 <= t - s < len(groups):
-                for c in groups[t - s]:
+    stages = [first_half]
+    lags = [0]
+    middle = [functools.partial(add, i) for i in range(bits - 1)]
+    middle += [update]
+    middle += [functools.partial(met, b) for b in range(tp_bits - 1)]
+    lags += [AHEAD + i for i in range(len(middle))]
+    tail = [select] + [functools.partial(forward, j) for j in range(bits)]
+    lags += [lags[-1] + 1 + LATE + i for i in range(len(tail))]
+    stages += middle + tail
+    for t in range(len(groups) + lags[-1]):
+        for lag, stage in zip(lags, stages):
+            if 0 <= t - lag < len(groups):
+                for c in groups[t - lag]:
                     stage(c)
 
     for c in range(chunks):
         raws[c].wait_send()
         for i in range(bits):
-            halving[c, i].wait_send()
+            for copy in halving[c, i]:
+                copy.wait_send()
             await_blocks(c, 1 << i, ag_s.at[c, i])
         for b in range(tp_bits):
             spread[c, b].wait_send()
         for sem in (fin_s, fin_r):
-            await_blocks(c, pairs, sem.at[c])
+            await_part(roll_ref.at[0, :, 0, 0], sem.at[c])
 
 
 def write_out(*refs):
@@ -367,13 +454,15 @@
 def fused(fsdp, tp, partials, token_counts, owner_map, params, moment1, moment2):
     layers, depth, width = partials.shape[1:]
     per = params.shape[1]
+    if per % (2 * TILE) or width % 256:
+        return plain(partials, token_counts, owner_map, params, moment1, moment2)
     pairs = fsdp // 2
     bits = pairs.bit_length() - 1
     tp_bits = tp.bit_length() - 1
-    parts = next(n for n in range(SPLIT, 0, -1) if per % (n * TILE) == 0)
+    parts = next(n for n in range(SPLIT, 0, -1) if per % (n * 2 * TILE) == 0)
     rows = per // parts
     chunks = layers * parts
-    weight = jnp.broadcast_to(token_counts.astype(jnp.float32)[:, None], (8, width))
+    lanes = 128
     anywhere = pl.BlockSpec(memory_space=pl.ANY)
     dma = pltpu.SemaphoreType.DMA
     state = (layers, parts, rows, width)
@@ -388,7 +477,7 @@
         ],
         in_specs=[
             pl.BlockSpec(memory_space=pltpu.SMEM),
-            pl.BlockSpec(memory_space=pltpu.VMEM),
+            pl.BlockSpec(memory_space=pltpu.SMEM),
             anywhere,
             anywhere,
             anywhere,
@@ -396,11 +485,15 @@
         ],
         out_specs=[pl.BlockSpec(memory_space=pltpu.VMEM)] * 4,
         scratch_shapes=[
-            pltpu.VMEM((fsdp, 8, width), f32),
+            pltpu.VMEM((8, lanes), f32),
+            pltpu.VMEM((fsdp, 8, lanes), f32),
             pltpu.VMEM((chunks, pairs, rows, width), b16),
             pltpu.VMEM((chunks, pairs, rows, width), b16),
-            pltpu.VMEM((chunks, pairs, rows, width), f32),
-            pltpu.VMEM((chunks, pairs, rows, width), f32),
+            pltpu.VMEM((chunks, pairs, rows, width), b16),
+            pltpu.VMEM((chunks, pairs, rows // 2, width // 2), jnp.int32),
+            pltpu.VMEM((chunks, pairs, rows, width), b16),
+            pltpu.VMEM((chunks, pairs, rows // 2, width // 2), jnp.int32),
+            pltpu.VMEM((chunks, pairs // 2, rows, width), f32),
             pltpu.VMEM((chunks, tp // 2, rows, width), b16),
             pltpu.VMEM((chunks, 2, rows, width), b16),
             dma((fsdp,)),
@@ -409,6 +502,8 @@
             dma((chunks,)),
             dma((chunks,)),
             dma((chunks,)),
+            dma((chunks, bits)),
+            dma((chunks, bits)),
             dma((chunks, bits)),
             dma((chunks, bits)),
             dma((chunks, tp_bits)),
@@ -423,7 +518,7 @@
         ),
     )(
         owner_map,
-        weight,
+        token_counts,
         partials.reshape(layers, pairs, 2, parts, rows, width),
         params.reshape(state),
         moment1.reshape(state),

time: 86.1 us -> 78.3 us (0.909)
  Pallas kernels: 84 us -> 76.8 us
    pallas_call x1, Pallas kernels: 80.3 us -> 73.1 us  [fused(): pl.pallas_call(functools.partial(kernel, (layers, fsdp, tp, parts, rows))...]
where the time goes in v2:
time: 78.3 us; the launch traced here: 78.1 us
  Pallas kernels  76.8 us (98%)
  between operations  1.29 us (2%)
    pallas_call x1, Pallas kernels, fused(): pl.pallas_call(functools.partial(kernel, (layers, fsdp, tp, parts, rows))...  73.1 us
    pallas_call x1, Pallas kernels, fused(): pl.pallas_call(write_out, out_shape=[jax.ShapeDtypeStruct(out.shape, out....  3.72 us

profile of v2, /device:TPU:0, one launch (start us, length us, event | category | flops | bytes accessed | tf_op | source)
XLA Modules:
  0.0 78.1 jit_solution(14558798751372052565)
XLA Ops:
  1.3 73.1 %shard_map.93 = (f32[2,10,64,256]{3,2,1,0:T(8,128)S(1)}, f32[2,10,64,256]{3,2,1,0:T(8,128)S(1)}, f32[2,10,64,256]{3,2,1,0:T(8,128)S(1)}, bf16[2,4,2,10,64,256]{5,4,3,2,1,0:T(8,128)(2,1)S(1)}) custom-call(s32[2,4]{1,0:T(2,128)} %owner_ref.1, s32[1]{0:T(128)S(6)} %copy.10.count_ref, bf16[2,4,2,10,64,256]{5,4,3,2,1,0:T(8,128)(2,1)} %bitcast.12, ...), custom_call_target="tpu_custom_call" | custom-call | tf_op jit(solution)/shard_map/pallas_call | solution.py:470
  74.4 3.7 %shard_map.94 = (f32[2,640,256]{2,1,0:T(8,128)}, f32[2,640,256]{2,1,0:T(8,128)}, f32[2,640,256]{2,1,0:T(8,128)}, bf16[2,5120,256]{2,1,0:T(8,128)(2,1)}) custom-call(f32[2,640,256]{2,1,0:T(8,128)S(1)} %bitcast.9, f32[2,640,256]{2,1,0:T(8,128)S(1)} %bitcast.10, f32[2,640,256]{2,1,0:T(8,128)S(1)} %bitcast.11, bf16[2,5120,256]{2,1,0:T(8,128)(2,1)S(1)} %bitcast.8), custom_call_target="tpu_custom_call" | custom-call | tf_op jit(solution)/shard_map/pallas_call | solution.py:529

commit v3 on v2

v3 whole, which is shorter than its diff:
```python
import functools

import jax
import jax.numpy as jnp
from jax import lax
from jax.experimental import pallas as pl
from jax.experimental.pallas import tpu as pltpu
from jax.sharding import PartitionSpec as P

STEP = 10
MESH = pl.DeviceIdType.MESH
SPLIT = 20
TILE = 16
SPAN = 80
AHEAD = 3
LATE = 6
GAP = 3
ZGAP = 3
AGAP = 4
CUTS = 5
LEVELS = 127
FINE = LEVELS * 256


def plain(partials, token_counts, owner_map, params, moment1, moment2):
    weight = token_counts.astype(jnp.float32)[0]
    total = lax.psum(weight, "fsdp")
    summed = lax.psum_scatter(
        weight * partials[0].astype(jnp.float32), "fsdp", scatter_dimension=1, tiled=True
    )
    first, second, direction, new_params = adam(summed * (1.0 / total), params, moment1, moment2)
    delta = direction.astype(jnp.bfloat16)
    owners = lax.axis_size("tp")
    served = lax.dynamic_index_in_dim(owner_map, lax.axis_index("tp"), 1, keepdims=False)
    blocks = lax.all_gather(delta, "tp", axis=0)
    kept = jnp.take_along_axis(blocks, served[None, :, None, None], axis=0)[0]
    rollout = lax.all_gather(kept, "fsdp", axis=1, tiled=True)
    return (new_params, first, second, rollout)


def adam(grad, params, moment1, moment2):
    first = 0.9 * moment1 + 0.1 * grad
    second = 0.999 * moment2 + 0.001 * grad * grad
    scale_one = 1.0 / (1.0 - 0.9**STEP)
    scale_two = 1.0 / (1.0 - 0.999**STEP)
    direction = first * scale_one / (jnp.sqrt(second * scale_two) + 1e-08)
    new_params = params - 0.001 * (direction + 0.1 * params)
    return first, second, direction, new_params


def code(value, high):
    rest = jnp.where(high == 0.0, 0.0, (value - high) * FINE / high)
    return (rest + (LEVELS + 1.5)).astype(jnp.int32)


def decode(high, number):
    return high + (number.astype(jnp.float32) - (LEVELS + 1.0)) * (high * (1.0 / FINE))


def kernel(
    sizes,
    owner_hbm,
    count_hbm,
    part_ref,
    p_ref,
    m_ref,
    v_ref,
    np_ref,
    nm_ref,
    nv_ref,
    roll_ref,
    owner_ref,
    count_ref,
    own_w,
    scale,
    wbuf,
    mine,
    theirs,
    near,
    out_hi,
    out_lo,
    in_hi,
    in_lo,
    acc,
    held,
    cross,
    in_s,
    w_s,
    w_r,
    opt_s,
    ld_s,
    raw_s,
    raw_r,
    near_s,
    near_r,
    hi_s,
    lo_s,
    rs_r,
    z_s,
    z_r,
    ag_s,
    ag_r,
    fin_s,
    fin_r,
):
    layers, fsdp, tp, parts, rows = sizes
    chunks = layers * parts
    pairs = fsdp // 2
    kept = pairs // 2
    bits = pairs.bit_length() - 1
    me = lax.axis_index("fsdp")
    col = lax.axis_index("tp")
    core = lax.rem(me, 2)
    mine_q = me // 2
    partner = mine_q * 2 + (1 - core)

    def away(index, flips):
        q = index
        for b in flips:
            q = q + (1 - 2 * lax.rem(index // (1 << b), 2)) * (1 << b)
        return q

    def ones(number):
        return [b for b in range(number.bit_length()) if number >> b & 1]

    tp_bits = tp.bit_length() - 1
    barrier = pltpu.get_barrier_semaphore()
    for d in range(1, fsdp):
        pl.semaphore_signal(
            barrier, inc=1, device_id={"fsdp": lax.rem(me + d, fsdp)}, device_id_type=MESH
        )
    for b in range(tp_bits):
        pl.semaphore_signal(
            barrier, inc=1, device_id={"tp": away(col, [b])}, device_id_type=MESH
        )

    groups = chunks // 2
    width = mine.shape[3]
    lanes = own_w.shape[1]

    def where(c):
        return lax.div(c, parts), lax.rem(c, parts)

    def order(slot):
        names = list(range(bits))
        return names if slot == 0 else names[::-1]

    def flipped(flips):
        return away(mine_q, flips)

    def block_of(slot, pos):
        return flipped([order(slot)[i] for i in range(bits) if pos >> (bits - 1 - i) & 1])

    def repeat(count, body):
        def run(i, carry):
            body(i)
            return carry

        lax.fori_loop(0, count, run, 0)

    def fetch(c):
        l, k = where(c)
        pltpu.make_async_copy(part_ref.at[l, :, core, k], mine.at[c], ld_s.at[0]).start()

    count_copy = pltpu.make_async_copy(count_hbm, count_ref, in_s.at[0])
    count_copy.start()
    owner_copy = pltpu.make_async_copy(owner_hbm, owner_ref, in_s.at[1])
    owner_copy.start()
    repeat(chunks, fetch)
    opts = []
    for i, (src, dst) in enumerate(((p_ref, np_ref), (m_ref, nm_ref), (v_ref, nv_ref))):
        load = pltpu.make_async_copy(src, dst, opt_s.at[i])
        load.start()
        opts.append(load)
    count_copy.wait()
    own_w[...] = jnp.full(own_w.shape, count_ref[0], jnp.int32).astype(jnp.float32)
    pl.semaphore_wait(barrier, fsdp - 1 + tp_bits)

    def push(src, dst, send, arrive, **device):
        pltpu.make_async_remote_copy(
            src_ref=src,
            dst_ref=dst,
            send_sem=send,
            recv_sem=arrive,
            device_id=device,
            device_id_type=MESH,
        ).start()

    def await_part(part, sem):
        pltpu.make_async_copy(part, part, sem).wait()

    for slot in range(2):
        l, k = slot // parts, slot % parts
        there = flipped([order(slot)[0]]) * 2
        for pos in range(kept):
            for half in range(2):
                push(
                    part_ref.at[l, block_of(slot, kept + pos), half, k],
                    near.at[slot, core, pos],
                    near_s.at[0],
                    near_r.at[0],
                    fsdp=there + half,
                )

    def share(c):
        l, k = where(c)
        push(
            part_ref.at[l, :, 1 - core, k],
            theirs.at[c],
            raw_s.at[0],
            raw_r.at[lax.div(c, 2)],
            fsdp=partner,
        )

    repeat(chunks, share)
    for d in range(1, fsdp):
        push(own_w, wbuf.at[d], w_s.at[0], w_r.at[min(d - 1, 1)], fsdp=away(me, ones(d)))

    def row(tile):
        return jnp.concatenate([tile[0:1, :]] * (width // lanes), axis=1)

    def weigh():
        await_part(wbuf.at[pl.ds(2, fsdp - 2)], w_r.at[1])
        total = own_w[...]
        for d in range(1, fsdp):
            total = total + wbuf[d]
        scale[...] = 1.0 / total

    side = rows // 2
    step = next(n for n in range(min(side, SPAN), 0, -TILE) if side % n == 0)

    def tiles(body):
        for i in range(0, rows, step):
            body(pl.ds(i, step))

    def quads(body):
        for i in range(0, side, step):
            body(pl.ds(i, step), pl.ds(i + side, step))

    def both(body):
        def run(g):
            for slot in range(2):
                body(2 * g + slot, slot)

        return run

    def halve(c, slot, i):
        half = pairs >> (i + 1)
        there = flipped([order(slot)[i]]) * 2 + core
        for src, dst, send in ((out_hi, in_hi, hi_s), (out_lo, in_lo, lo_s)):
            push(
                src.at[c, pl.ds(half, half)],
                dst.at[c, pl.ds(half, half)],
                send.at[i],
                rs_r.at[lax.div(c, 2), i],
                fsdp=there,
            )

    def arrived(g, i):
        half = pairs >> (i + 1)
        tall, wide = (2, 3 * half // 2) if half > 1 else (3, 1)
        await_part(mine.at[pl.ds(0, tall), pl.ds(0, wide)], rs_r.at[g, i])

    def pair_sum(c, slot, pos, at):
        q = block_of(slot, pos)
        own = row(own_w[...]) * mine[c, q, at, :].astype(jnp.float32)
        return own + row(wbuf[1]) * theirs[c, q, at, :].astype(jnp.float32)

    def near_sum(slot, pos, at):
        index = 1 << (order(slot)[0] + 1)
        total = row(wbuf[index + core]) * near[slot, 0, pos, at, :].astype(jnp.float32)
        return total + row(wbuf[index + 1 - core]) * near[slot, 1, pos, at, :].astype(jnp.float32)

    def write(c, pos, at, pair, values):
        numbers = []
        for rows_at, value in zip(pair, values):
            high = value.astype(jnp.bfloat16)
            out_hi[c, pos, rows_at, :] = high
            number = code(value, high.astype(jnp.float32))
            numbers += [number[:, : width // 2], number[:, width // 2 :]]
        word = numbers[0]
        for n in range(1, 4):
            word = word | (numbers[n] << (8 * n))
        out_lo[c, pos, at, :] = word

    def read(c, pos, at, pair):
        word = in_lo[c, pos, at, :]
        numbers = [(word >> (8 * n)) & 255 for n in range(4)]
        return [
            decode(
                in_hi[c, pos, rows_at, :].astype(jnp.float32),
                jnp.concatenate(numbers[2 * n : 2 * n + 2], axis=1),
            )
            for n, rows_at in enumerate(pair)
        ]

    def held_rows(c, slot, pos):
        q = flipped([order(slot)[b] for b in ones(pos)])
        l, k = where(c)
        return roll_ref.at[l, q, core, k]

    def double(c, slot, j):
        there = flipped([order(slot)[j]]) * 2 + core
        for pos in range(1 << j):
            block = held_rows(c, slot, pos)
            push(block, block, ag_s.at[j], ag_r.at[lax.div(c, 2), j], fsdp=there)

    def pair_of(g):
        return pl.ds(2 * g, 2)

    def first_halves(g):
        await_part(theirs.at[pair_of(g)], raw_r.at[g])

        @pl.when(g == 0)
        def _():
            await_part(mine, ld_s.at[0])
            await_part(wbuf.at[1], w_r.at[0])

        @pl.when(g > 0)
        def _():
            both(first_half)(g)

    def first_half(c, slot):
        for pos in range(pairs - 1, kept - 1, -1):

            def body(*pair):
                write(c, pos, pair[0], pair, [pair_sum(c, slot, pos, at) for at in pair])

            quads(body)
        halve(c, slot, 0)

    def adds(i, g):
        if i > 0:
            arrived(g, i)
            both(functools.partial(add, i, False))(g)
            return

        @pl.when(g == 0)
        def _():
            await_part(near, near_r.at[0])
            weigh()
            both(functools.partial(add, i, True))(g)

        @pl.when(g > 0)
        def _():
            arrived(g, i)
            both(functools.partial(add, i, False))(g)

    def add(i, raw, c, slot):
        half = pairs >> (i + 1)
        for pos in range(half - 1, -1, -1):

            def body(*pair):
                if raw:
                    totals = [near_sum(slot, pos, at) for at in pair]
                else:
                    totals = read(c, half + pos, pair[0], pair)
                for n, at in enumerate(pair):
                    totals[n] += pair_sum(c, slot, pos, at) if i == 0 else acc[c, pos, at, :]
                if half > 1 and pos >= half // 2:
                    write(c, pos, pair[0], pair, totals)
                else:
                    for at, total in zip(pair, totals):
                        acc[c, pos, at, :] = total

            quads(body)
            if half > 1 and pos == half // 2:
                halve(c, slot, i + 1)

    def updates(g):
        @pl.when(g == 0)
        def _():
            for load in opts:
                load.wait()
            owner_copy.wait()

        arrived(g, bits - 1)
        both(update)(g)

    def update(c, slot):
        l, k = where(c)

        def body(*pair):
            totals = read(c, 1, pair[0], pair)
            for at, total in zip(pair, totals):
                total = total + acc[c, 0, at, :]
                first, second, direction, new_params = adam(
                    total * row(scale[...]),
                    np_ref[l, k, at, :],
                    nm_ref[l, k, at, :],
                    nv_ref[l, k, at, :],
                )
                held[c, 0, at, :] = direction.astype(jnp.bfloat16)
                np_ref[l, k, at, :] = new_params
                nm_ref[l, k, at, :] = first
                nv_ref[l, k, at, :] = second

        quads(body)
        if tp_bits > 1:
            meet(c, 0)
        else:
            hand_over(c, slot)

    def meet(c, b):
        size = 1 << b
        push(
            held.at[c, pl.ds(0, size)],
            held.at[c, pl.ds(size, size)],
            z_s.at[b],
            z_r.at[lax.div(c, 2), b],
            tp=away(col, [b]),
        )

    def pick(c, at, served, start):
        chosen = start
        for slot in range(tp // 2):
            chosen = jnp.where(
                served == away(col, ones(slot)), held[c, slot, at, :].astype(jnp.float32), chosen
            )
        return chosen.astype(jnp.bfloat16)

    def hand_over(c, slot):
        l, k = where(c)
        there = away(col, [tp_bits - 1])
        served = owner_ref[l, there]

        def body(at):
            cross[c, 0, at, :] = pick(c, at, served, held[c, 0, at, :].astype(jnp.float32))

        tiles(body)
        push(
            cross.at[c, 0],
            cross.at[c, 1],
            z_s.at[tp_bits - 1],
            z_r.at[lax.div(c, 2), tp_bits - 1],
            tp=there,
        )

    def met(b, g):
        size = 1 << b
        await_part(held.at[pair_of(g), pl.ds(size, size)], z_r.at[g, b])
        if b + 2 < tp_bits:
            for slot in range(2):
                meet(2 * g + slot, b + 1)
        else:
            both(hand_over)(g)

    def selects(g):
        await_part(cross.at[pair_of(g), 1], z_r.at[g, tp_bits - 1])
        both(select)(g)

    def select(c, slot):
        l, k = where(c)
        served = owner_ref[l, col]

        def body(at):
            roll_ref[l, mine_q, core, k, at, :] = pick(
                c, at, served, cross[c, 1, at, :].astype(jnp.float32)
            )

        tiles(body)
        double(c, slot, 0)
        finish(c, slot, 0, 1)

    def finish(c, slot, first, count):
        for pos in range(first, first + count):
            block = held_rows(c, slot, pos)
            push(block, block, fin_s.at[0], fin_r.at[0], fsdp=partner)

    def forward(j, g):
        await_part(mine.at[pl.ds(0, 2), pl.ds(0, 1 << j)], ag_r.at[g, j])
        for slot in range(2):
            if j + 1 < bits:
                double(2 * g + slot, slot, j + 1)
            finish(2 * g + slot, slot, 1 << j, 1 << j)

    stages = [first_halves]
    lags = [0]
    middle = [functools.partial(adds, i) for i in range(bits - 1)]
    middle += [updates]
    middle += [functools.partial(met, b) for b in range(tp_bits - 1)]
    lags += [AHEAD + GAP * i for i in range(bits)]
    lags += [lags[-1] + ZGAP * (b + 1) for b in range(tp_bits - 1)]
    tail = [selects] + [functools.partial(forward, j) for j in range(bits)]
    lags += [lags[-1] + LATE + AGAP * i for i in range(len(tail))]
    stages += middle + tail

    def at_step(t):
        for lag, stage in zip(lags, stages):
            g = t - lag
            pl.when(jnp.logical_and(g >= 0, g < groups))(functools.partial(stage, g))

    repeat(groups + lags[-1], at_step)

    await_part(wbuf.at[pl.ds(1, fsdp - 1)], w_s.at[0])
    await_part(theirs, raw_s.at[0])
    await_part(near, near_s.at[0])
    for i in range(bits):
        half = pairs >> (i + 1)
        sent = chunks if i > 0 else chunks - 2
        await_part(out_hi.at[pl.ds(0, sent), pl.ds(0, half)], hi_s.at[i])
        await_part(out_lo.at[pl.ds(0, sent), pl.ds(0, half)], lo_s.at[i])
        await_part(mine.at[:, pl.ds(0, 1 << i)], ag_s.at[i])
    for b in range(tp_bits - 1):
        await_part(held.at[:, pl.ds(0, 1 << b)], z_s.at[b])
    await_part(cross.at[:, 0], z_s.at[tp_bits - 1])
    for sem in (fin_s, fin_r):
        await_part(mine, sem.at[0])


def write_out(*refs):
    count = len(refs) // 2
    copies = []
    for i in range(count):
        n = refs[i].shape[1] // CUTS
        for l in range(refs[i].shape[0]):
            for j in range(CUTS):
                at = (l, pl.ds(j * n, n))
                copies.append(
                    pltpu.make_async_copy(refs[i].at[at], refs[count + i].at[at], refs[-1].at[i])
                )
    for copy in copies:
        copy.start()
    for i in range(count):
        pltpu.make_async_copy(refs[i], refs[count + i], refs[-1].at[i]).wait()


def fused(fsdp, tp, partials, token_counts, owner_map, params, moment1, moment2):
    layers, depth, width = partials.shape[1:]
    per = params.shape[1]
    pairs = fsdp // 2
    bits = pairs.bit_length() - 1
    tp_bits = tp.bit_length() - 1
    parts = next((n for n in range(SPLIT, 0, -1) if per % (n * 2 * TILE) == 0), None)
    if parts is None or width % 256 or layers * parts % 2 or layers * parts < 4:
        return plain(partials, token_counts, owner_map, params, moment1, moment2)
    rows = per // parts
    chunks = layers * parts
    lanes = 128
    anywhere = pl.BlockSpec(memory_space=pl.ANY)
    dma = pltpu.SemaphoreType.DMA
    state = (layers, parts, rows, width)
    f32, b16 = jnp.float32, jnp.bfloat16
    outs = pl.pallas_call(
        functools.partial(kernel, (layers, fsdp, tp, parts, rows)),
        out_shape=[
            pltpu.VMEM(state, f32),
            pltpu.VMEM(state, f32),
            pltpu.VMEM(state, f32),
            pltpu.VMEM((layers, pairs, 2, parts, rows, width), b16),
        ],
        in_specs=[
            anywhere,
            anywhere,
            anywhere,
            anywhere,
            anywhere,
            anywhere,
        ],
        out_specs=[pl.BlockSpec(memory_space=pltpu.VMEM)] * 4,
        scratch_shapes=[
            pltpu.SMEM((layers, tp), jnp.int32),
            pltpu.SMEM((1,), jnp.int32),
            pltpu.VMEM((8, lanes), f32),
            pltpu.VMEM((8, lanes), f32),
            pltpu.VMEM((fsdp, 8, lanes), f32),
            pltpu.VMEM((chunks, pairs, rows, width), b16),
            pltpu.VMEM((chunks, pairs, rows, width), b16),
            pltpu.VMEM((2, 2, pairs // 2, rows, width), b16),
            pltpu.VMEM((chunks, pairs, rows, width), b16),
            pltpu.VMEM((chunks, pairs, rows // 2, width // 2), jnp.int32),
            pltpu.VMEM((chunks, pairs, rows, width), b16),
            pltpu.VMEM((chunks, pairs, rows // 2, width // 2), jnp.int32),
            pltpu.VMEM((chunks, pairs // 2, rows, width), f32),
            pltpu.VMEM((chunks, tp // 2, rows, width), b16),
            pltpu.VMEM((chunks, 2, rows, width), b16),
            dma((2,)),
            dma((1,)),
            dma((2,)),
            dma((3,)),
            dma((1,)),
            dma((1,)),
            dma((chunks // 2,)),
            dma((1,)),
            dma((1,)),
            dma((bits,)),
            dma((bits,)),
            dma((chunks // 2, bits)),
            dma((tp_bits,)),
            dma((chunks // 2, tp_bits)),
            dma((bits,)),
            dma((chunks // 2, bits)),
            dma((1,)),
            dma((1,)),
        ],
        compiler_params=pltpu.CompilerParams(
            collective_id=0, has_side_effects=True, vmem_limit_bytes=48 * 1024 * 1024
        ),
    )(
        owner_map,
        token_counts,
        partials.reshape(layers, pairs, 2, parts, rows, width),
        params.reshape(state),
        moment1.reshape(state),
        moment2.reshape(state),
    )
    outs = [out.reshape(params.shape) for out in outs[:3]] + [outs[3].reshape(layers, depth, width)]
    return tuple(
        pl.pallas_call(
            write_out,
            out_shape=[jax.ShapeDtypeStruct(out.shape, out.dtype) for out in outs],
            in_specs=[pl.BlockSpec(memory_space=pltpu.VMEM)] * 4,
            out_specs=[anywhere] * 4,
            scratch_shapes=[dma((4,))],
            compiler_params=pltpu.CompilerParams(vmem_limit_bytes=16 * 1024 * 1024),
        )(*outs)
    )


def solution(mesh):
    fsdp, tp = mesh.shape["fsdp"], mesh.shape["tp"]
    local = plain
    if fsdp >= 8 and fsdp & (fsdp - 1) == 0 and tp > 1 and tp & (tp - 1) == 0:
        local = functools.partial(fused, fsdp, tp)
    in_specs = (
        P("fsdp", None, None, "tp"),
        P("fsdp"),
        P(),
        P(None, "fsdp", "tp"),
        P(None, "fsdp", "tp"),
        P(None, "fsdp", "tp"),
    )
    out_specs = (
        P(None, "fsdp", "tp"),
        P(None, "fsdp", "tp"),
        P(None, "fsdp", "tp"),
        P(None, None, "tp"),
    )
    return jax.shard_map(local, mesh=mesh, in_specs=in_specs, out_specs=out_specs, check_vma=False)
```

time: 78.3 us -> 71 us (0.907)
  Pallas kernels: 76.8 us -> 69.6 us
    pallas_call x1, Pallas kernels: 73.1 us -> 66.1 us  [fused(): pl.pallas_call(functools.partial(kernel, (layers, fsdp, tp, parts, rows))...]
where the time goes in v3:
time: 71 us; the launch traced here: 70.9 us
  Pallas kernels  69.6 us (98%)
  between operations  1.29 us (2%)
    pallas_call x1, Pallas kernels, fused(): pl.pallas_call(functools.partial(kernel, (layers, fsdp, tp, parts, rows))...  66.1 us
    pallas_call x1, Pallas kernels, fused(): pl.pallas_call(write_out, out_shape=[jax.ShapeDtypeStruct(out.shape, out....  3.54 us

profile of v3, /device:TPU:0, one launch (start us, length us, event | category | flops | bytes accessed | tf_op | source)
XLA Modules:
  0.0 70.9 jit_solution(2750065723466196826)
XLA Ops:
  1.3 66.1 %shard_map.93 = (f32[2,20,32,256]{3,2,1,0:T(8,128)S(1)}, f32[2,20,32,256]{3,2,1,0:T(8,128)S(1)}, f32[2,20,32,256]{3,2,1,0:T(8,128)S(1)}, bf16[2,4,2,20,32,256]{5,4,3,2,1,0:T(8,128)(2,1)S(1)}) custom-call(s32[2,4]{1,0:T(2,128)} %owner_hbm.1, s32[1]{0:T(128)S(6)} %copy.10.count_hbm, bf16[2,4,2,20,32,256]{5,4,3,2,1,0:T(8,128)(2,1)} %bitcast.12, ...), custom_call_target="tpu_custom_call" | custom-call | tf_op jit(solution)/shard_map/pallas_call | solution.py:544
  67.3 3.5 %shard_map.94 = (f32[2,640,256]{2,1,0:T(8,128)}, f32[2,640,256]{2,1,0:T(8,128)}, f32[2,640,256]{2,1,0:T(8,128)}, bf16[2,5120,256]{2,1,0:T(8,128)(2,1)}) custom-call(f32[2,640,256]{2,1,0:T(8,128)S(1)} %bitcast.9, f32[2,640,256]{2,1,0:T(8,128)S(1)} %bitcast.10, f32[2,640,256]{2,1,0:T(8,128)S(1)} %bitcast.11, bf16[2,5120,256]{2,1,0:T(8,128)(2,1)S(1)} %bitcast.8), custom_call_target="tpu_custom_call" | custom-call | tf_op jit(solution)/shard_map/pallas_call | solution.py:609

commit v4 on v3

--- a/solution.py
+++ b/solution.py
@@ -18,8 +18,10 @@
 ZGAP = 3
 AGAP = 4
 CUTS = 5
-LEVELS = 127
-FINE = LEVELS * 256
+OCTAVES = 40
+CODES = 1 << 19
+FINE = CODES / OCTAVES
+LARGEST = 12
 
 
 def plain(partials, token_counts, owner_map, params, moment1, moment2):
@@ -48,13 +50,17 @@
     return first, second, direction, new_params
 
 
-def code(value, high):
-    rest = jnp.where(high == 0.0, 0.0, (value - high) * FINE / high)
-    return (rest + (LEVELS + 1.5)).astype(jnp.int32)
-
-
-def decode(high, number):
-    return high + (number.astype(jnp.float32) - (LEVELS + 1.0)) * (high * (1.0 / FINE))
+def code(value, top):
+    level = (jnp.log2(jnp.abs(value)) + (OCTAVES - top)) * FINE
+    number = (jnp.clip(level, 0.0, CODES - 1.0) + 0.5).astype(jnp.int32)
+    return jnp.where(value < 0.0, number + CODES, number)
+
+
+def decode(number, top):
+    level = number & (CODES - 1)
+    size = jnp.exp2(level.astype(jnp.float32) * (1.0 / FINE) - (OCTAVES - top))
+    size = jnp.where(level == 0, 0.0, size)
+    return jnp.where(number >= CODES, -size, size)
 
 
 def kernel(
@@ -135,6 +141,7 @@
         )
 
     groups = chunks // 2
+    top = LARGEST + fsdp.bit_length() - 1
     width = mine.shape[3]
     lanes = own_w.shape[1]
 
@@ -258,8 +265,7 @@
 
     def arrived(g, i):
         half = pairs >> (i + 1)
-        tall, wide = (2, 3 * half // 2) if half > 1 else (3, 1)
-        await_part(mine.at[pl.ds(0, tall), pl.ds(0, wide)], rs_r.at[g, i])
+        await_part(in_lo.at[pl.ds(0, 5), pl.ds(0, 2 * half)], rs_r.at[g, i])
 
     def pair_sum(c, slot, pos, at):
         q = block_of(slot, pos)
@@ -271,28 +277,31 @@
         total = row(wbuf[index + core]) * near[slot, 0, pos, at, :].astype(jnp.float32)
         return total + row(wbuf[index + 1 - core]) * near[slot, 1, pos, at, :].astype(jnp.float32)
 
-    def write(c, pos, at, pair, values):
-        numbers = []
-        for rows_at, value in zip(pair, values):
-            high = value.astype(jnp.bfloat16)
-            out_hi[c, pos, rows_at, :] = high
-            number = code(value, high.astype(jnp.float32))
-            numbers += [number[:, : width // 2], number[:, width // 2 :]]
-        word = numbers[0]
-        for n in range(1, 4):
-            word = word | (numbers[n] << (8 * n))
-        out_lo[c, pos, at, :] = word
-
-    def read(c, pos, at, pair):
-        word = in_lo[c, pos, at, :]
-        numbers = [(word >> (8 * n)) & 255 for n in range(4)]
-        return [
-            decode(
-                in_hi[c, pos, rows_at, :].astype(jnp.float32),
-                jnp.concatenate(numbers[2 * n : 2 * n + 2], axis=1),
-            )
-            for n, rows_at in enumerate(pair)
-        ]
+    def fine_rows(at):
+        return pl.ds(at.start // 2, at.size // 2)
+
+    def write(c, pos, pair, values):
+        numbers = [code(value, top) for value in values]
+        out_hi[c, pos, pair[0], :] = (numbers[0] >> 4) | ((numbers[1] >> 4) << 16)
+        middle, half = step // 2, width // 2
+        word = None
+        for n, number in enumerate(numbers):
+            low = number & 15
+            low = low[:middle] | (low[middle:] << 4)
+            low = (low[:, :half] | (low[:, half:] << 8)) << (16 * n)
+            word = low if word is None else word | low
+        out_lo[c, pos, fine_rows(pair[0]), :] = word
+
+    def read(c, pos, pair):
+        high = in_hi[c, pos, pair[0], :]
+        word = in_lo[c, pos, fine_rows(pair[0]), :]
+        values = []
+        for n in range(2):
+            low = (word >> (16 * n)) & 65535
+            low = jnp.concatenate([low & 255, low >> 8], axis=1)
+            low = jnp.concatenate([low & 15, low >> 4], axis=0)
+            values.append(decode((((high >> (16 * n)) & 65535) << 4) | low, top))
+        return values
 
     def held_rows(c, slot, pos):
         q = flipped([order(slot)[b] for b in ones(pos)])
@@ -324,7 +333,7 @@
         for pos in range(pairs - 1, kept - 1, -1):
 
             def body(*pair):
-                write(c, pos, pair[0], pair, [pair_sum(c, slot, pos, at) for at in pair])
+                write(c, pos, pair, [pair_sum(c, slot, pos, at) for at in pair])
 
             quads(body)
         halve(c, slot, 0)
@@ -354,11 +363,11 @@
                 if raw:
                     totals = [near_sum(slot, pos, at) for at in pair]
                 else:
-                    totals = read(c, half + pos, pair[0], pair)
+                    totals = read(c, half + pos, pair)
                 for n, at in enumerate(pair):
                     totals[n] += pair_sum(c, slot, pos, at) if i == 0 else acc[c, pos, at, :]
                 if half > 1 and pos >= half // 2:
-                    write(c, pos, pair[0], pair, totals)
+                    write(c, pos, pair, totals)
                 else:
                     for at, total in zip(pair, totals):
                         acc[c, pos, at, :] = total
@@ -381,7 +390,7 @@
         l, k = where(c)
 
         def body(*pair):
-            totals = read(c, 1, pair[0], pair)
+            totals = read(c, 1, pair)
             for at, total in zip(pair, totals):
                 total = total + acc[c, 0, at, :]
                 first, second, direction, new_params = adam(
@@ -532,7 +541,7 @@
     bits = pairs.bit_length() - 1
     tp_bits = tp.bit_length() - 1
     parts = next((n for n in range(SPLIT, 0, -1) if per % (n * 2 * TILE) == 0), None)
-    if parts is None or width % 256 or layers * parts % 2 or layers * parts < 4:
+    if parts is None or width % 256 or layers * parts % 2 or layers * parts < 5:
         return plain(partials, token_counts, owner_map, params, moment1, moment2)
     rows = per // parts
     chunks = layers * parts
@@ -567,10 +576,10 @@
             pltpu.VMEM((chunks, pairs, rows, width), b16),
             pltpu.VMEM((chunks, pairs, rows, width), b16),
             pltpu.VMEM((2, 2, pairs // 2, rows, width), b16),
-            pltpu.VMEM((chunks, pairs, rows, width), b16),
-            pltpu.VMEM((chunks, pairs, rows // 2, width // 2), jnp.int32),
-            pltpu.VMEM((chunks, pairs, rows, width), b16),
-            pltpu.VMEM((chunks, pairs, rows // 2, width // 2), jnp.int32),
+            pltpu.VMEM((chunks, pairs, rows // 2, width), jnp.int32),
+            pltpu.VMEM((chunks, pairs, rows // 4, width // 2), jnp.int32),
+            pltpu.VMEM((chunks, pairs, rows // 2, width), jnp.int32),
+            pltpu.VMEM((chunks, pairs, rows // 4, width // 2), jnp.int32),
             pltpu.VMEM((chunks, pairs // 2, rows, width), f32),
             pltpu.VMEM((chunks, tp // 2, rows, width), b16),
             pltpu.VMEM((chunks, 2, rows, width), b16),

time: 71 us -> 66 us (0.930)
  Pallas kernels: 69.6 us -> 64.6 us
    pallas_call x1, Pallas kernels: 66.1 us -> 61 us  [fused(): pl.pallas_call(functools.partial(kernel, (layers, fsdp, tp, parts, rows))...]
where the time goes in v4:
time: 66 us; the launch traced here: 65.8 us
  Pallas kernels  64.6 us (98%)
  between operations  1.29 us (2%)
    pallas_call x1, Pallas kernels, fused(): pl.pallas_call(functools.partial(kernel, (layers, fsdp, tp, parts, rows))...  61 us
    pallas_call x1, Pallas kernels, fused(): pl.pallas_call(write_out, out_shape=[jax.ShapeDtypeStruct(out.shape, out....  3.54 us

profile of v4, /device:TPU:0, one launch (start us, length us, event | category | flops | bytes accessed | tf_op | source)
XLA Modules:
  0.0 65.8 jit_solution(10279459663723673484)
XLA Ops:
  1.3 61.0 %shard_map.93 = (f32[2,20,32,256]{3,2,1,0:T(8,128)S(1)}, f32[2,20,32,256]{3,2,1,0:T(8,128)S(1)}, f32[2,20,32,256]{3,2,1,0:T(8,128)S(1)}, bf16[2,4,2,20,32,256]{5,4,3,2,1,0:T(8,128)(2,1)S(1)}) custom-call(s32[2,4]{1,0:T(2,128)} %owner_hbm.1, s32[1]{0:T(128)S(6)} %copy.10.count_hbm, bf16[2,4,2,20,32,256]{5,4,3,2,1,0:T(8,128)(2,1)} %bitcast.12, ...), custom_call_target="tpu_custom_call" | custom-call | tf_op jit(solution)/shard_map/pallas_call | solution.py:553
  62.3 3.5 %shard_map.94 = (f32[2,640,256]{2,1,0:T(8,128)}, f32[2,640,256]{2,1,0:T(8,128)}, f32[2,640,256]{2,1,0:T(8,128)}, bf16[2,5120,256]{2,1,0:T(8,128)(2,1)}) custom-call(f32[2,640,256]{2,1,0:T(8,128)S(1)} %bitcast.9, f32[2,640,256]{2,1,0:T(8,128)S(1)} %bitcast.10, f32[2,640,256]{2,1,0:T(8,128)S(1)} %bitcast.11, bf16[2,5120,256]{2,1,0:T(8,128)(2,1)S(1)} %bitcast.8), custom_call_target="tpu_custom_call" | custom-call | tf_op jit(solution)/shard_map/pallas_call | solution.py:618

commit v5 on v4

--- a/solution.py
+++ b/solution.py
@@ -18,7 +18,7 @@
 ZGAP = 3
 AGAP = 4
 CUTS = 5
-OCTAVES = 40
+OCTAVES = 36
 CODES = 1 << 19
 FINE = CODES / OCTAVES
 LARGEST = 12
@@ -80,7 +80,7 @@
     own_w,
     scale,
     wbuf,
-    mine,
+    block,
     theirs,
     near,
     out_hi,
@@ -142,7 +142,7 @@
 
     groups = chunks // 2
     top = LARGEST + fsdp.bit_length() - 1
-    width = mine.shape[3]
+    width = theirs.shape[3]
     lanes = own_w.shape[1]
 
     def where(c):
@@ -165,20 +165,18 @@
 
         lax.fori_loop(0, count, run, 0)
 
-    def fetch(c):
+    def fetch(c, sem):
         l, k = where(c)
-        pltpu.make_async_copy(part_ref.at[l, :, core, k], mine.at[c], ld_s.at[0]).start()
+        pltpu.make_async_copy(part_ref.at[l, :, :, k], block.at[c], ld_s.at[sem]).start()
 
     count_copy = pltpu.make_async_copy(count_hbm, count_ref, in_s.at[0])
     count_copy.start()
     owner_copy = pltpu.make_async_copy(owner_hbm, owner_ref, in_s.at[1])
     owner_copy.start()
-    repeat(chunks, fetch)
-    opts = []
-    for i, (src, dst) in enumerate(((p_ref, np_ref), (m_ref, nm_ref), (v_ref, nv_ref))):
-        load = pltpu.make_async_copy(src, dst, opt_s.at[i])
-        load.start()
-        opts.append(load)
+    early = 4
+    for c in range(early):
+        fetch(c, c // 2)
+    repeat(chunks - early, lambda i: fetch(i + early, 2))
     count_copy.wait()
     own_w[...] = jnp.full(own_w.shape, count_ref[0], jnp.int32).astype(jnp.float32)
     pl.semaphore_wait(barrier, fsdp - 1 + tp_bits)
@@ -196,13 +194,13 @@
     def await_part(part, sem):
         pltpu.make_async_copy(part, part, sem).wait()
 
+    await_part(block.at[pl.ds(0, 2)], ld_s.at[0])
     for slot in range(2):
-        l, k = slot // parts, slot % parts
         there = flipped([order(slot)[0]]) * 2
         for pos in range(kept):
             for half in range(2):
                 push(
-                    part_ref.at[l, block_of(slot, kept + pos), half, k],
+                    block.at[slot, block_of(slot, kept + pos), half],
                     near.at[slot, core, pos],
                     near_s.at[0],
                     near_r.at[0],
@@ -210,18 +208,27 @@
                 )
 
     def share(c):
-        l, k = where(c)
         push(
-            part_ref.at[l, :, 1 - core, k],
+            block.at[c, :, 1 - core],
             theirs.at[c],
             raw_s.at[0],
             raw_r.at[lax.div(c, 2)],
             fsdp=partner,
         )
 
-    repeat(chunks, share)
+    for c in range(early):
+        if c == 2:
+            await_part(block.at[pl.ds(2, 2)], ld_s.at[1])
+        share(c)
     for d in range(1, fsdp):
         push(own_w, wbuf.at[d], w_s.at[0], w_r.at[min(d - 1, 1)], fsdp=away(me, ones(d)))
+    await_part(block.at[pl.ds(early, chunks - early)], ld_s.at[2])
+    repeat(chunks - early, lambda i: share(i + early))
+    opts = []
+    for i, (src, dst) in enumerate(((p_ref, np_ref), (m_ref, nm_ref), (v_ref, nv_ref))):
+        load = pltpu.make_async_copy(src, dst, opt_s.at[i])
+        load.start()
+        opts.append(load)
 
     def row(tile):
         return jnp.concatenate([tile[0:1, :]] * (width // lanes), axis=1)
@@ -269,7 +276,7 @@
 
     def pair_sum(c, slot, pos, at):
         q = block_of(slot, pos)
-        own = row(own_w[...]) * mine[c, q, at, :].astype(jnp.float32)
+        own = row(own_w[...]) * block[c, q, core, at, :].astype(jnp.float32)
         return own + row(wbuf[1]) * theirs[c, q, at, :].astype(jnp.float32)
 
     def near_sum(slot, pos, at):
@@ -322,7 +329,6 @@
 
         @pl.when(g == 0)
         def _():
-            await_part(mine, ld_s.at[0])
             await_part(wbuf.at[1], w_r.at[0])
 
         @pl.when(g > 0)
@@ -477,7 +483,7 @@
             push(block, block, fin_s.at[0], fin_r.at[0], fsdp=partner)
 
     def forward(j, g):
-        await_part(mine.at[pl.ds(0, 2), pl.ds(0, 1 << j)], ag_r.at[g, j])
+        await_part(theirs.at[pl.ds(0, 2), pl.ds(0, 1 << j)], ag_r.at[g, j])
         for slot in range(2):
             if j + 1 < bits:
                 double(2 * g + slot, slot, j + 1)
@@ -509,12 +515,12 @@
         sent = chunks if i > 0 else chunks - 2
         await_part(out_hi.at[pl.ds(0, sent), pl.ds(0, half)], hi_s.at[i])
         await_part(out_lo.at[pl.ds(0, sent), pl.ds(0, half)], lo_s.at[i])
-        await_part(mine.at[:, pl.ds(0, 1 << i)], ag_s.at[i])
+        await_part(theirs.at[:, pl.ds(0, 1 << i)], ag_s.at[i])
     for b in range(tp_bits - 1):
         await_part(held.at[:, pl.ds(0, 1 << b)], z_s.at[b])
     await_part(cross.at[:, 0], z_s.at[tp_bits - 1])
     for sem in (fin_s, fin_r):
-        await_part(mine, sem.at[0])
+        await_part(theirs, sem.at[0])
 
 
 def write_out(*refs):
@@ -573,7 +579,7 @@
             pltpu.VMEM((8, lanes), f32),
             pltpu.VMEM((8, lanes), f32),
             pltpu.VMEM((fsdp, 8, lanes), f32),
-            pltpu.VMEM((chunks, pairs, rows, width), b16),
+            pltpu.VMEM((chunks, pairs, 2, rows, width), b16),
             pltpu.VMEM((chunks, pairs, rows, width), b16),
             pltpu.VMEM((2, 2, pairs // 2, rows, width), b16),
             pltpu.VMEM((chunks, pairs, rows // 2, width), jnp.int32),
@@ -587,7 +593,7 @@
             dma((1,)),
             dma((2,)),
             dma((3,)),
-            dma((1,)),
+            dma((3,)),
             dma((1,)),
             dma((chunks // 2,)),
             dma((1,)),

time: 66 us -> 62.4 us (0.945)
  Pallas kernels: 64.6 us -> 61 us
    pallas_call x1, Pallas kernels: 61 us -> 57.4 us  [fused(): pl.pallas_call(functools.partial(kernel, (layers, fsdp, tp, parts, rows))...]
where the time goes in v5:
time: 62.4 us; the launch traced here: 62.2 us
  Pallas kernels  61 us (98%)
  between operations  1.29 us (2%)
    pallas_call x1, Pallas kernels, fused(): pl.pallas_call(functools.partial(kernel, (layers, fsdp, tp, parts, rows))...  57.4 us
    pallas_call x1, Pallas kernels, fused(): pl.pallas_call(write_out, out_shape=[jax.ShapeDtypeStruct(out.shape, out....  3.54 us

profile of v5, /device:TPU:0, one launch (start us, length us, event | category | flops | bytes accessed | tf_op | source)
XLA Modules:
  0.0 62.2 jit_solution(2590493829602479392)
XLA Ops:
  1.3 57.4 %shard_map.93 = (f32[2,20,32,256]{3,2,1,0:T(8,128)S(1)}, f32[2,20,32,256]{3,2,1,0:T(8,128)S(1)}, f32[2,20,32,256]{3,2,1,0:T(8,128)S(1)}, bf16[2,4,2,20,32,256]{5,4,3,2,1,0:T(8,128)(2,1)S(1)}) custom-call(s32[2,4]{1,0:T(2,128)} %owner_hbm.1, s32[1]{0:T(128)S(6)} %copy.10.count_hbm, bf16[2,4,2,20,32,256]{5,4,3,2,1,0:T(8,128)(2,1)} %bitcast.12, ...), custom_call_target="tpu_custom_call" | custom-call | tf_op jit(solution)/shard_map/pallas_call | solution.py:559
  58.7 3.5 %shard_map.94 = (f32[2,640,256]{2,1,0:T(8,128)}, f32[2,640,256]{2,1,0:T(8,128)}, f32[2,640,256]{2,1,0:T(8,128)}, bf16[2,5120,256]{2,1,0:T(8,128)(2,1)}) custom-call(f32[2,640,256]{2,1,0:T(8,128)S(1)} %bitcast.9, f32[2,640,256]{2,1,0:T(8,128)S(1)} %bitcast.10, f32[2,640,256]{2,1,0:T(8,128)S(1)} %bitcast.11, bf16[2,5120,256]{2,1,0:T(8,128)(2,1)S(1)} %bitcast.8), custom_call_target="tpu_custom_call" | custom-call | tf_op jit(solution)/shard_map/pallas_call | solution.py:624

commit v6 on v5

--- a/solution.py
+++ b/solution.py
@@ -18,6 +18,8 @@
 ZGAP = 3
 AGAP = 4
 CUTS = 5
+RING = 12
+SINGLE = 6
 OCTAVES = 36
 CODES = 1 << 19
 FINE = CODES / OCTAVES
@@ -104,6 +106,7 @@
     rs_r,
     z_s,
     z_r,
+    last_r,
     ag_s,
     ag_r,
     fin_s,
@@ -158,6 +161,9 @@
     def block_of(slot, pos):
         return flipped([order(slot)[i] for i in range(bits) if pos >> (bits - 1 - i) & 1])
 
+    def turn(g):
+        return lax.rem(g, min(RING, groups))
+
     def repeat(count, body):
         def run(i, carry):
             body(i)
@@ -207,12 +213,14 @@
                     fsdp=there + half,
                 )
 
+    single = min(SINGLE, groups - 1)
+
     def share(c):
         push(
             block.at[c, :, 1 - core],
             theirs.at[c],
             raw_s.at[0],
-            raw_r.at[lax.div(c, 2)],
+            raw_r.at[jnp.minimum(lax.div(c, 2), single)],
             fsdp=partner,
         )
 
@@ -266,13 +274,13 @@
                 src.at[c, pl.ds(half, half)],
                 dst.at[c, pl.ds(half, half)],
                 send.at[i],
-                rs_r.at[lax.div(c, 2), i],
+                rs_r.at[turn(lax.div(c, 2)), i],
                 fsdp=there,
             )
 
     def arrived(g, i):
         half = pairs >> (i + 1)
-        await_part(in_lo.at[pl.ds(0, 5), pl.ds(0, 2 * half)], rs_r.at[g, i])
+        await_part(in_lo.at[pl.ds(0, 5), pl.ds(0, 2 * half)], rs_r.at[turn(g), i])
 
     def pair_sum(c, slot, pos, at):
         q = block_of(slot, pos)
@@ -319,13 +327,20 @@
         there = flipped([order(slot)[j]]) * 2 + core
         for pos in range(1 << j):
             block = held_rows(c, slot, pos)
-            push(block, block, ag_s.at[j], ag_r.at[lax.div(c, 2), j], fsdp=there)
+            push(block, block, ag_s.at[j], ag_r.at[turn(lax.div(c, 2)), j], fsdp=there)
 
     def pair_of(g):
         return pl.ds(2 * g, 2)
 
     def first_halves(g):
-        await_part(theirs.at[pair_of(g)], raw_r.at[g])
+        @pl.when(g < single)
+        def _():
+            await_part(theirs.at[pair_of(g)], raw_r.at[g])
+
+        @pl.when(g == single)
+        def _():
+            first = 2 * single
+            await_part(theirs.at[pl.ds(first, chunks - first)], raw_r.at[single])
 
         @pl.when(g == 0)
         def _():
@@ -422,7 +437,7 @@
             held.at[c, pl.ds(0, size)],
             held.at[c, pl.ds(size, size)],
             z_s.at[b],
-            z_r.at[lax.div(c, 2), b],
+            z_r.at[turn(lax.div(c, 2)), b],
             tp=away(col, [b]),
         )
 
@@ -447,13 +462,13 @@
             cross.at[c, 0],
             cross.at[c, 1],
             z_s.at[tp_bits - 1],
-            z_r.at[lax.div(c, 2), tp_bits - 1],
+            last_r.at[lax.div(c, 2)],
             tp=there,
         )
 
     def met(b, g):
         size = 1 << b
-        await_part(held.at[pair_of(g), pl.ds(size, size)], z_r.at[g, b])
+        await_part(held.at[pair_of(g), pl.ds(size, size)], z_r.at[turn(g), b])
         if b + 2 < tp_bits:
             for slot in range(2):
                 meet(2 * g + slot, b + 1)
@@ -461,7 +476,7 @@
             both(hand_over)(g)
 
     def selects(g):
-        await_part(cross.at[pair_of(g), 1], z_r.at[g, tp_bits - 1])
+        await_part(cross.at[pair_of(g), 1], last_r.at[g])
         both(select)(g)
 
     def select(c, slot):
@@ -483,7 +498,7 @@
             push(block, block, fin_s.at[0], fin_r.at[0], fsdp=partner)
 
     def forward(j, g):
-        await_part(theirs.at[pl.ds(0, 2), pl.ds(0, 1 << j)], ag_r.at[g, j])
+        await_part(theirs.at[pl.ds(0, 2), pl.ds(0, 1 << j)], ag_r.at[turn(g), j])
         for slot in range(2):
             if j + 1 < bits:
                 double(2 * g + slot, slot, j + 1)
@@ -551,6 +566,7 @@
         return plain(partials, token_counts, owner_map, params, moment1, moment2)
     rows = per // parts
     chunks = layers * parts
+    ring = min(RING, chunks // 2)
     lanes = 128
     anywhere = pl.BlockSpec(memory_space=pl.ANY)
     dma = pltpu.SemaphoreType.DMA
@@ -595,16 +611,17 @@
             dma((3,)),
             dma((3,)),
             dma((1,)),
-            dma((chunks // 2,)),
+            dma((min(SINGLE + 1, chunks // 2),)),
             dma((1,)),
             dma((1,)),
             dma((bits,)),
             dma((bits,)),
-            dma((chunks // 2, bits)),
+            dma((ring, bits)),
             dma((tp_bits,)),
-            dma((chunks // 2, tp_bits)),
+            dma((ring, max(tp_bits - 1, 1))),
+            dma((chunks // 2,)),
             dma((bits,)),
-            dma((chunks // 2, bits)),
+            dma((ring, bits)),
             dma((1,)),
             dma((1,)),
         ],

time: 62.4 us -> 61.9 us (level)
  no operation moved by 1% of the time
where the time goes in v6:
time: 61.9 us; the launch traced here: 61.8 us
  Pallas kernels  60.5 us (98%)
  between operations  1.29 us (2%)
    pallas_call x1, Pallas kernels, fused(): pl.pallas_call(functools.partial(kernel, (layers, fsdp, tp, parts, rows))...  56.9 us
    pallas_call x1, Pallas kernels, fused(): pl.pallas_call(write_out, out_shape=[jax.ShapeDtypeStruct(out.shape, out....  3.54 us

profile of v6, /device:TPU:0, one launch (start us, length us, event | category | flops | bytes accessed | tf_op | source)
XLA Modules:
  0.0 61.8 jit_solution(17449121851149529493)
XLA Ops:
  1.3 56.9 %shard_map.93 = (f32[2,20,32,256]{3,2,1,0:T(8,128)S(1)}, f32[2,20,32,256]{3,2,1,0:T(8,128)S(1)}, f32[2,20,32,256]{3,2,1,0:T(8,128)S(1)}, bf16[2,4,2,20,32,256]{5,4,3,2,1,0:T(8,128)(2,1)S(1)}) custom-call(s32[2,4]{1,0:T(2,128)} %owner_hbm.1, s32[1]{0:T(128)S(6)} %copy.10.count_hbm, bf16[2,4,2,20,32,256]{5,4,3,2,1,0:T(8,128)(2,1)} %bitcast.12, ...), custom_call_target="tpu_custom_call" | custom-call | tf_op jit(solution)/shard_map/pallas_call | solution.py:575
  58.2 3.5 %shard_map.94 = (f32[2,640,256]{2,1,0:T(8,128)}, f32[2,640,256]{2,1,0:T(8,128)}, f32[2,640,256]{2,1,0:T(8,128)}, bf16[2,5120,256]{2,1,0:T(8,128)(2,1)}) custom-call(f32[2,640,256]{2,1,0:T(8,128)S(1)} %bitcast.9, f32[2,640,256]{2,1,0:T(8,128)S(1)} %bitcast.10, f32[2,640,256]{2,1,0:T(8,128)S(1)} %bitcast.11, bf16[2,5120,256]{2,1,0:T(8,128)(2,1)S(1)} %bitcast.8), custom_call_target="tpu_custom_call" | custom-call | tf_op jit(solution)/shard_map/pallas_call | solution.py:641

commit v7 on v6

--- a/solution.py
+++ b/solution.py
@@ -18,8 +18,8 @@
 ZGAP = 3
 AGAP = 4
 CUTS = 5
-RING = 12
-SINGLE = 6
+RING = 10
+SINGLE = 4
 OCTAVES = 36
 CODES = 1 << 19
 FINE = CODES / OCTAVES
@@ -183,8 +183,6 @@
     for c in range(early):
         fetch(c, c // 2)
     repeat(chunks - early, lambda i: fetch(i + early, 2))
-    count_copy.wait()
-    own_w[...] = jnp.full(own_w.shape, count_ref[0], jnp.int32).astype(jnp.float32)
     pl.semaphore_wait(barrier, fsdp - 1 + tp_bits)
 
     def push(src, dst, send, arrive, **device):
@@ -224,6 +222,8 @@
             fsdp=partner,
         )
 
+    count_copy.wait()
+    own_w[...] = jnp.full(own_w.shape, count_ref[0], jnp.int32).astype(jnp.float32)
     for c in range(early):
         if c == 2:
             await_part(block.at[pl.ds(2, 2)], ld_s.at[1])

time: 61.9 us -> 61.7 us (level)
  no operation moved by 1% of the time
where the time goes in v7:
time: 61.7 us; the launch traced here: 61.6 us
  Pallas kernels  60.3 us (98%)
  between operations  1.29 us (2%)
    pallas_call x1, Pallas kernels, fused(): pl.pallas_call(functools.partial(kernel, (layers, fsdp, tp, parts, rows))...  56.8 us
    pallas_call x1, Pallas kernels, fused(): pl.pallas_call(write_out, out_shape=[jax.ShapeDtypeStruct(out.shape, out....  3.54 us

profile of v7, /device:TPU:0, one launch (start us, length us, event | category | flops | bytes accessed | tf_op | source)
XLA Modules:
  0.0 61.6 jit_solution(9043905499406001869)
XLA Ops:
  1.3 56.8 %shard_map.93 = (f32[2,20,32,256]{3,2,1,0:T(8,128)S(1)}, f32[2,20,32,256]{3,2,1,0:T(8,128)S(1)}, f32[2,20,32,256]{3,2,1,0:T(8,128)S(1)}, bf16[2,4,2,20,32,256]{5,4,3,2,1,0:T(8,128)(2,1)S(1)}) custom-call(s32[2,4]{1,0:T(2,128)} %owner_hbm.1, s32[1]{0:T(128)S(6)} %copy.10.count_hbm, bf16[2,4,2,20,32,256]{5,4,3,2,1,0:T(8,128)(2,1)} %bitcast.12, ...), custom_call_target="tpu_custom_call" | custom-call | tf_op jit(solution)/shard_map/pallas_call | solution.py:575
  58.0 3.5 %shard_map.94 = (f32[2,640,256]{2,1,0:T(8,128)}, f32[2,640,256]{2,1,0:T(8,128)}, f32[2,640,256]{2,1,0:T(8,128)}, bf16[2,5120,256]{2,1,0:T(8,128)(2,1)}) custom-call(f32[2,640,256]{2,1,0:T(8,128)S(1)} %bitcast.9, f32[2,640,256]{2,1,0:T(8,128)S(1)} %bitcast.10, f32[2,640,256]{2,1,0:T(8,128)S(1)} %bitcast.11, bf16[2,5120,256]{2,1,0:T(8,128)(2,1)S(1)} %bitcast.8), custom_call_target="tpu_custom_call" | custom-call | tf_op jit(solution)/shard_map/pallas_call | solution.py:641
